TPU v7x, 32 devices: a whole 2x2x4 slice. The times are simulated.
32 devices in a mesh: dp: 8 (over y, x, core), mp: 4 (over z).
Axes of the slice: x: 2, y: 2, z: 4, core: 2. Of those that a mesh axis runs over, the one named last changes fastest.
Arguments:
- grad_parts: bfloat16 [8, 1, 6144, 6144], P('dp', None, None, 'mp'), may hold values from -6 to 6
- master: float32 [1, 6144, 6144], P(None, 'dp', 'mp'), may hold values from -6 to 6
- momentum: float32 [1, 6144, 6144], P(None, 'dp', 'mp'), may hold values from -4 to 4
Outputs:
- new_master: float32 [1, 6144, 6144], P(None, 'dp', 'mp')
- new_momentum: float32 [1, 6144, 6144], P(None, 'dp', 'mp')
- new_weights: bfloat16 [1, 6144, 6144], P(None, None, 'mp')
All inputs are finite; a program needn't handle non-finite values.
Results may differ from a plain program's by a relative error of at most 0.0014.
Values may be sent and summed in bfloat16 or wider, within the bound.
No kernel may reach another device: no remote copies, remote signals or barrier semaphores. Data moves between devices by JAX's collectives and lax.ppermute only.
A program may use at most 128 MiB of HBM per device.

v0:
```python
import jax
import jax.numpy as jnp
from jax import lax
from jax.sharding import PartitionSpec as P

beta_one = 0.9
beta_two = 0.99
step_size = 0.1
decay_rate = 0.1
softness = 0.05


def lion_update(gradient, master, momentum):
    interp = beta_one * momentum + (1.0 - beta_one) * gradient
    direction = interp / jnp.sqrt(interp * interp + softness * softness)
    new_master = master - step_size * (direction + decay_rate * master)
    new_momentum = beta_two * momentum + (1.0 - beta_two) * gradient
    return (new_master, new_momentum)


def per_device(grad_parts, master, momentum):
    replicas = lax.axis_size("dp")
    partials = grad_parts[0].astype(jnp.float32)
    summed = lax.psum_scatter(
        partials.astype(jnp.bfloat16), "dp", scatter_dimension=1, tiled=True
    ).astype(jnp.float32)
    gradient = summed / replicas
    new_master, new_momentum = lion_update(gradient, master, momentum)
    new_weights = lax.all_gather(new_master.astype(jnp.bfloat16), "dp", axis=1, tiled=True)
    return (new_master, new_momentum, new_weights)


def solution(mesh):
    return jax.shard_map(
        per_device,
        mesh=mesh,
        in_specs=(P("dp", None, None, "mp"), P(None, "dp", "mp"), P(None, "dp", "mp")),
        out_specs=(P(None, "dp", "mp"), P(None, "dp", "mp"), P(None, None, "mp")),
        check_vma=False,
    )
```

profile of v0, /device:TPU:0, one launch (start us, length us, event | category | flops | bytes accessed | tf_op | source)
XLA Modules:
  0.0 271.5 jit_solution(14277638528274021986)
XLA Ops:
  7.2 0.0 reduce-scatter.2.cloned.1.call-start
  7.2 0.7 reduce-scatter.2.cloned.1.call-update
  7.9 0.0 all-gather.2.cloned.1.call-start
  7.9 132.9 %reduce-scatter.2.cloned.1.call-done = bf16[1,768,1536]{2,1,0:T(8,128)(2,1)} async-done(((bf16[1,6144,1536]{2,1,0:T(8,128)(2,1)}), bf16[1,768,1536]{2,1,0:T(8,128)(2,1)}) %reduce-scatter.2.cloned.1.call-update) | async-done | bytes 2359312 | tf_op jit(solution)/shard_map/reduce_scatter | solution.py:24
  140.8 8.7 %fusion.2 = (bf16[1,768,1536]{2,1,0:T(8,128)(2,1)}, f32[1,768,1536]{2,1,0:T(8,128)}, f32[1,768,1536]{2,1,0:T(8,128)}) fusion(f32[1,768,1536]{2,1,0:T(8,128)} %param.4, bf16[1,768,1536]{2,1,0:T(8,128)(2,1)} %reduce-scatter.2.cloned.1.call-done, f32[1,768,1536]{2,1,0:T(8,128)} %param.5), kind=kLoop, calls=%fused_computation.5 | loop fusion | flops 17694720 | bytes 23592960 | tf_op jit(solution)/shard_map/convert_element_type | solution.py:29
  149.5 0.0 all-gather.2.cloned.1.call-update
  149.5 98.7 %all-gather.2.cloned.1.call-done = bf16[1,6144,1536]{2,1,0:T(8,128)(2,1)} async-done(((bf16[1,768,1536]{2,1,0:T(8,128)(2,1)}), bf16[1,6144,1536]{2,1,0:T(8,128)(2,1)}) %all-gather.2.cloned.1.call-update) | async-done | bytes 18874384 | tf_op jit(solution)/shard_map/all_gather | solution.py:29
  248.2 16.5 %copy.7 = bf16[1,6144,1536]{2,1,0:T(8,128)(2,1)} copy(bf16[1,6144,1536]{2,1,0:T(8,128)(2,1)} %all-gather.2.cloned.1.call-done) | data formatting | bytes 37748736
Async XLA Ops:
  7.2 133.6 %reduce-scatter.2.cloned.1.call-start = ((), (), s32[]{:S(2)}) async-start(), calls=%async_computation.1 | async-start | bytes 21233664 | tf_op jit(solution)/shard_map/reduce_scatter | solution.py:24
  7.9 240.3 %all-gather.2.cloned.1.call-start = ((), (), s32[]{:S(2)}) async-start(), calls=%async_computation.2 | async-start | bytes 21233664 | tf_op jit(solution)/shard_map/all_gather | solution.py:29
Sparse Core Ops, SparseCore 0:
  11.6 129.1 reduce-scatter.1
  149.6 98.5 all-gather.1
where the time goes:
time: 272 us
  waiting for transfers between devices  232 us (85%)
  local copies, waits for them, and re-layouts  16.5 us (6%)
  between operations  14 us (5%)
  other arithmetic  8.67 us (3%)
    reduce_scatter x1, waiting for transfers between devices, per_device(): lax.psum_scatter(partials.astype(jnp.bfloat16), 'dp', scatter_dimension=1...  133 us
    all_gather x1, waiting for transfers between devices, per_device(): lax.all_gather(new_master.astype(jnp.bfloat16), 'dp', axis=1, tiled=True)  98.7 us
    unnamed x1, local copies, waits for them, and re-layouts  16.5 us
    convert_element_type x1, other arithmetic, per_device(): new_master.astype(jnp.bfloat16)  8.67 us
  transfers between devices with their start and end apart: 2, of which 2 were waited for; matrix products, arithmetic and copies ran while one was open for 0% of the time, Pallas kernels for 0%

commit v1 on v0

v1 whole, which is shorter than its diff:
```python
import functools

import jax
import jax.numpy as jnp
from jax import lax
from jax.experimental import pallas as pl
from jax.experimental.pallas import tpu as pltpu
from jax.sharding import PartitionSpec as P


beta_one = 0.9
beta_two = 0.99
step_size = 0.1
decay_rate = 0.1
softness = 0.05

UNITS = 8
CHUNKS = (1, 2, 2, 2, 1)
VMEM_LIMIT = 8 << 20


def lion_update(gradient, master, momentum):
    interp = beta_one * momentum + (1.0 - beta_one) * gradient
    direction = interp * lax.rsqrt(interp * interp + softness * softness)
    new_master = master - step_size * (direction + decay_rate * master)
    new_momentum = beta_two * momentum + (1.0 - beta_two) * gradient
    return (new_master, new_momentum)


def per_device_collectives(grad_parts, master, momentum):
    replicas = lax.axis_size("dp")
    summed = lax.psum_scatter(grad_parts[0], "dp", scatter_dimension=1, tiled=True)
    gradient = summed.astype(jnp.float32) / replicas
    new_master, new_momentum = lion_update(gradient, master, momentum)
    new_weights = lax.all_gather(new_master.astype(jnp.bfloat16), "dp", axis=1, tiled=True)
    return (new_master, new_momentum, new_weights)


ROWS = 16


def rows_loop(rows, body):
    @pl.loop(0, rows // ROWS)
    def _(i):
        body(pl.multiple_of(i * ROWS, ROWS))


def at(ref, row, rows=ROWS):
    return ref.at[pl.ds(row, rows), :]


def f32(ref, row):
    return ref[pl.ds(row, ROWS), :].astype(jnp.float32)


def cut_kernel(rows, row0, tile, s_ref, raw_ref, out_ref, sem):
    mine = 1 - s_ref[0] % 2
    copies = [
        pltpu.make_async_copy(at(raw_ref, (2 * m + mine) * tile + row0, rows), at(out_ref, m * rows, rows), sem.at[m])
        for m in range(4)
    ]
    for c in copies:
        c.start()
    for c in copies:
        c.wait()


def combine_kernel(rows, row0, tile, s_ref, raw_ref, peer_ref, out_ref, raw, sem):
    copies = [
        pltpu.make_async_copy(at(raw_ref, s_ref[1 + 2 * j] * tile + row0, rows), at(raw, j * rows, rows), sem.at[j])
        for j in range(2)
    ]
    for c in copies:
        c.start()
    for j, c in enumerate(copies):
        base = (s_ref[1 + 2 * j] // 2) * rows
        c.wait()

        def body(row):
            total = f32(raw, j * rows + row) + f32(peer_ref, base + row)
            out_ref[pl.ds(j * rows + row, ROWS), :] = total.astype(jnp.bfloat16)

        rows_loop(rows, body)


def second_kernel(rows, row0, tile, s_ref, raw_ref, peer_ref, recv_ref, out_ref, raw, sem):
    copy = pltpu.make_async_copy(at(raw_ref, s_ref[2] * tile + row0, rows), raw, sem)
    copy.start()
    base = (s_ref[2] // 2) * rows
    copy.wait()

    def body(row):
        total = f32(raw, row) + f32(peer_ref, base + row) + f32(recv_ref, rows + row)
        out_ref[pl.ds(row, ROWS), :] = total.astype(jnp.bfloat16)

    rows_loop(rows, body)


def update_kernel(rows, row0, tile, scale, s_ref, raw_ref, peer_ref, first_ref, second_ref, master_ref, momentum_ref, *rest):
    new_master_ref, new_momentum_ref, weights_ref, raw, mas, mom, sem = rest[-7:]
    loads = [
        pltpu.make_async_copy(at(raw_ref, s_ref[0] * tile + row0, rows), raw, sem.at[0]),
        pltpu.make_async_copy(at(master_ref, row0, rows), mas, sem.at[1]),
        pltpu.make_async_copy(at(momentum_ref, row0, rows), mom, sem.at[2]),
    ]
    for c in loads:
        c.start()
    base = (s_ref[0] // 2) * rows
    for c in loads:
        c.wait()

    def body(row):
        summed = (f32(raw, row) + f32(peer_ref, base + row)) + (f32(first_ref, row) + f32(second_ref, row))
        here = pl.ds(row, ROWS)
        new_master, new_momentum = lion_update(summed * scale, mas[here, :], mom[here, :])
        mas[here, :] = new_master
        mom[here, :] = new_momentum
        weights_ref[here, :] = new_master.astype(jnp.bfloat16)

    rows_loop(rows, body)
    stores = [
        pltpu.make_async_copy(mas, at(new_master_ref, row0, rows), sem.at[1]),
        pltpu.make_async_copy(mom, at(new_momentum_ref, row0, rows), sem.at[2]),
    ]
    for c in stores:
        c.start()
    for c in stores:
        c.wait()


def place_kernel(count, rows, row0, tile, s_ref, *refs):
    sources, out_ref, sem = refs[:count], refs[-2], refs[-1]
    copies = [
        pltpu.make_async_copy(src, at(out_ref, s_ref[i] * tile + row0, rows), sem.at[i])
        for i, src in enumerate(sources)
    ]
    for c in copies:
        c.start()
    for c in copies:
        c.wait()


def per_device(grad_parts, master, momentum):
    replicas = lax.axis_size("dp")
    _, _, total_rows, cols = grad_parts.shape
    tile = total_rows // replicas
    if replicas != 8 or tile % UNITS or (tile // UNITS) % 16:
        return per_device_collectives(grad_parts, master, momentum)
    rb = tile // UNITS
    bf = jnp.bfloat16

    grad = grad_parts.reshape(total_rows, cols)
    master = master.reshape(tile, cols)
    momentum = momentum.reshape(tile, cols)
    me = lax.axis_index("dp")
    core = me & 1
    first = jnp.where(core == 0, 2, 4)
    second = 6 - first

    t_first, t_second, t_both = me ^ first, me ^ second, me ^ 6
    scal = jnp.stack([me, t_first, t_second, t_both]).astype(jnp.int32)
    place_a = jnp.stack([me, t_second, t_first, me ^ 1, me ^ 1 ^ first, me ^ 1 ^ second]).astype(jnp.int32)
    place_f = jnp.stack([t_both, me ^ 1 ^ 6]).astype(jnp.int32)

    def first_bit(i):
        return 4 if i & 1 else 2

    along_first = [(i, i ^ first_bit(i)) for i in range(replicas)]
    along_second = [(i, i ^ 6 ^ first_bit(i)) for i in range(replicas)]
    across = [(i, i ^ 1) for i in range(replicas)]

    def permute(x, perm):
        return lax.ppermute(x, "dp", perm)

    starts, row = [], 0
    for n in CHUNKS:
        starts.append(row)
        row += n * rb
    K = len(CHUNKS)

    def vmem(rows):
        return pltpu.VMEM((rows, cols), bf)

    def call(kernel, k, tiles, far, close, out_shape, scratch, aliases=None):
        any_spec = pl.BlockSpec(memory_space=pltpu.HBM)
        vmem_spec = pl.BlockSpec(memory_space=pltpu.VMEM)
        outs = out_shape if isinstance(out_shape, list) else [out_shape]
        specs = [vmem_spec if o.dtype == bf and o.shape[0] != total_rows else any_spec for o in outs]
        return pl.pallas_call(
            functools.partial(kernel, CHUNKS[k] * rb, starts[k], tile),
            grid_spec=pltpu.PrefetchScalarGridSpec(
                num_scalar_prefetch=1,
                grid=(),
                in_specs=[vmem_spec if c else any_spec for c in close],
                out_specs=specs if isinstance(out_shape, list) else specs[0],
                scratch_shapes=scratch,
            ),
            out_shape=out_shape,
            input_output_aliases=aliases or {},
            compiler_params=pltpu.CompilerParams(vmem_limit_bytes=VMEM_LIMIT),
        )(tiles, *[pltpu.with_memory_space_constraint(x, pltpu.VMEM if c else pltpu.HBM) for x, c in zip(far, close)])

    def dma(*n):
        return pltpu.SemaphoreType.DMA(n)

    def cut(k):
        rows = CHUNKS[k] * rb
        return call(cut_kernel, k, scal, [grad], [0], vmem(4 * rows), [dma(4)])

    def combine(k, peer):
        rows = CHUNKS[k] * rb
        return call(combine_kernel, k, scal, [grad, peer], [0, 1], vmem(2 * rows), [vmem(2 * rows), dma(2)])

    def second_combine(k, peer, recv):
        rows = CHUNKS[k] * rb
        return call(second_kernel, k, scal, [grad, peer, recv], [0, 1, 1], vmem(rows), [vmem(rows), dma()])

    def update(k, peer, recv, recv2, carried):
        rows = CHUNKS[k] * rb
        full = pltpu.HBM((tile, cols), jnp.float32)
        part = pltpu.VMEM((rows, cols), jnp.float32)
        extra = [] if carried is None else list(carried)
        kernel = lambda r, r0, t, *refs: update_kernel(r, r0, t, 1.0 / replicas, *refs)
        return call(
            kernel,
            k,
            scal,
            [grad, peer, recv, recv2, master, momentum] + extra,
            [0, 1, 1, 1, 0, 0] + [0] * len(extra),
            [full, full, vmem(rows)],
            [vmem(rows), part, part, dma(3)],
            {7: 0, 8: 1} if extra else {},
        )

    def place(k, tiles, sources, weights):
        count = len(sources)
        extra = [] if weights is None else [weights]
        kernel = functools.partial(place_kernel, count)
        return call(
            kernel,
            k,
            tiles,
            list(sources) + extra,
            [1] * count + [0] * len(extra),
            pltpu.HBM((total_rows, cols), bf),
            [dma(count)],
            {count + 1: 0} if extra else {},
        )

    peers, got, got2 = [None] * K, [None] * K, [None] * K
    for k in range(K):
        raw = cut(k)
        peers[k] = permute(raw, across)
        part = combine(k, peers[k])
        got[k] = permute(part, along_first)
    for k in range(K):
        part = second_combine(k, peers[k], got[k])
        got2[k] = permute(part, along_second)
    carried = None
    weights = None
    for k in range(K):
        new_master, new_momentum, own = update(k, peers[k], got[k], got2[k], carried)
        carried = (new_master, new_momentum)
        a = permute(own, along_second)
        b = permute(own, along_first)
        f = permute(a, along_first)
        own1 = permute(own, across)
        a1 = permute(a, across)
        b1 = permute(b, across)
        f1 = permute(f, across)
        weights = place(k, place_a, [own, a, b, own1, a1, b1], weights)
        weights = place(k, place_f, [f, f1], weights)
    shape = (1, tile, cols)
    return (carried[0].reshape(shape), carried[1].reshape(shape), weights.reshape(1, total_rows, cols))


def solution(mesh):
    return jax.shard_map(
        per_device,
        mesh=mesh,
        in_specs=(P("dp", None, None, "mp"), P(None, "dp", "mp"), P(None, "dp", "mp")),
        out_specs=(P(None, "dp", "mp"), P(None, "dp", "mp"), P(None, None, "mp")),
        check_vma=False,
    )
```

time: 272 us -> 217 us (0.80)
  waiting for transfers between devices: 232 us -> 82.5 us
  Pallas kernels: 0 us -> 72.5 us
  starting transfers between devices: 0.08 us -> 36.8 us
  between operations: 14 us -> 1.3 us
  other arithmetic: 8.67 us -> 0.15 us
  local copies, waits for them, and re-layouts: 16.5 us -> 22.8 us
    reduce_scatter x1 -> x0, waiting for transfers between devices: 133 us -> none  [per_device(): lax.psum_scatter(partials.astype(jnp.bfloat16), 'dp', scatter_dimension=1...]
    all_gather x1 -> x0, waiting for transfers between devices: 98.7 us -> none  [per_device(): lax.all_gather(new_master.astype(jnp.bfloat16), 'dp', axis=1, tiled=True)]
    ppermute x0 -> x50, waiting for transfers between devices: none -> 82.5 us  [permute(): return lax.ppermute(x, 'dp', perm)]
    pallas_call x0 -> x30, Pallas kernels: none -> 72.5 us  [call(): pl.pallas_call(functools.partial(kernel, CHUNKS[k] * rb, starts[k], tile)...]
    ppermute x0 -> x50, starting transfers between devices: none -> 36.8 us  [permute(): return lax.ppermute(x, 'dp', perm)]
    convert_element_type x1 -> x0, other arithmetic: 8.67 us -> none  [per_device(): new_master.astype(jnp.bfloat16)]
    unnamed x1 -> x96, local copies, waits for them, and re-layouts: 16.5 us -> 22.8 us
  transfers between devices with their start and end apart: 2 -> 50, of which waited for: 2 -> 14; matrix products, arithmetic and copies ran while one was open for 0% -> 0% of each run, Pallas kernels for 0% -> 31%
where the time goes in v1:
time: 217 us; the launch traced here: 216 us
  waiting for transfers between devices  82.5 us (38%)
  Pallas kernels  72.5 us (33%)
  starting transfers between devices  36.8 us (17%)
  local copies, waits for them, and re-layouts  22.8 us (11%)
    ppermute x50, waiting for transfers between devices, permute(): return lax.ppermute(x, 'dp', perm)  82.5 us
    pallas_call x30, Pallas kernels, call(): pl.pallas_call(functools.partial(kernel, CHUNKS[k] * rb, starts[k], tile)...  72.5 us
    ppermute x50, starting transfers between devices, permute(): return lax.ppermute(x, 'dp', perm)  36.8 us
    unnamed x96, local copies, waits for them, and re-layouts  22.8 us
  transfers between devices with their start and end apart: 50, of which 14 were waited for; matrix products, arithmetic and copies ran while one was open for 0% of the time, Pallas kernels for 31%

profile of v1, /device:TPU:0, one launch (start us, length us, event | category | flops | bytes accessed | tf_op | source)
XLA Modules:
  0.0 216.0 jit_solution(13577804621604620817)
XLA Ops:
  0.7 2.2 %shard_map.67 = bf16[768,1536]{1,0:T(8,128)(2,1)S(1)} custom-call(s32[4]{0:T(128)S(1)} %pad_add_fusion.s_ref.refs_0_, bf16[6144,1536]{1,0:T(8,128)(2,1)} %bitcast.14), custom_call_target="tpu_custom_call" | custom-call | tf_op jit(solution)/shard_map/pallas_call | solution.py:189
  14.8 2.6 %collective-permute-start.10 = (bf16[384,1536]{1,0:T(8,128)(2,1)S(1)}, bf16[384,1536]{1,0:T(8,128)(2,1)S(1)}, u32[]{:S(2)}, u32[]{:S(2)}) collective-permute-start(bf16[384,1536]{1,0:T(8,128)(2,1)S(1)} %shard_map.68), channel_id=1, source_target_pairs={{0,8},{4,20},{8,0},{12,28},{16,24},{20,4},{24,16},{28,12},{1,9},{5... | collective-permute-start | bytes 3538952 | tf_op jit(solution)/shard_map/ppermute | solution.py:173
  25.5 25.1 %collective-permute-done.13.recv_ref.refs_3_ = bf16[192,1536]{1,0:T(8,128)(2,1)S(1)} collective-permute-done((bf16[192,1536]{1,0:T(8,128)(2,1)S(1)}, bf16[192,1536]{1,0:T(8,128)(2,1)S(1)}, u32[]{:S(2)}, u32[]{:S(2)}) %collective-permute-start.13) | collective-permute-done | bytes 589856 | tf_op jit(solution)/shard_map/ppermute | solution.py:173
  57.6 4.6 %collective-permute-done.14.refs_4_ = bf16[96,1536]{1,0:T(8,128)(2,1)S(1)} collective-permute-done((bf16[96,1536]{1,0:T(8,128)(2,1)S(1)}, bf16[96,1536]{1,0:T(8,128)(2,1)S(1)}, u32[]{:S(2)}, u32[]{:S(2)}) %collective-permute-start.14) | collective-permute-done | bytes 294944 | tf_op jit(solution)/shard_map/ppermute | solution.py:173
  62.2 3.4 %shard_map.73 = (f32[768,1536]{1,0:T(8,128)}, f32[768,1536]{1,0:T(8,128)}, bf16[96,1536]{1,0:T(8,128)(2,1)S(1)}) custom-call(s32[4]{0:T(128)S(1)} %pad_add_fusion.s_ref.refs_0_, bf16[6144,1536]{1,0:T(8,128)(2,1)} %bitcast.25, bf16[384,1536]{1,0:T(8,128)(2,1)S(1)} %collective-permute-done.12.peer_ref.refs_2_, ...), custom_call_target="tpu_custom_call" | custom-call | tf_op jit(solution)/shard_map/pallas_call | solution.py:189
  75.6 2.4 %collective-permute-done.1.recv_ref.refs_3_ = bf16[192,1536]{1,0:T(8,128)(2,1)S(1)} collective-permute-done((bf16[192,1536]{1,0:T(8,128)(2,1)S(1)}, bf16[192,1536]{1,0:T(8,128)(2,1)S(1)}, u32[]{:S(2)}, u32[]{:S(2)}) %collective-permute-start.1) | collective-permute-done | bytes 589856 | tf_op jit(solution)/shard_map/ppermute | solution.py:173
  78.0 2.3 %collective-permute-start.46 = (bf16[96,1536]{1,0:T(8,128)(2,1)S(1)}, bf16[96,1536]{1,0:T(8,128)(2,1)S(1)}, u32[]{:S(2)}, u32[]{:S(2)}) collective-permute-start(bf16[96,1536]{1,0:T(8,128)(2,1)S(1)} %get-tuple-element.32.refs_0_), channel_id=1, source_target_pairs={{0,8},{4,20},{8,0},{12,28},{16,24},{20,4},{24,16},{28,12},{1,9},{5... | collective-permute-start | bytes 884744 | tf_op jit(solution)/shard_map/ppermute | solution.py:173
  82.0 6.1 %collective-permute-done.46.refs_2_ = bf16[96,1536]{1,0:T(8,128)(2,1)S(1)} collective-permute-done((bf16[96,1536]{1,0:T(8,128)(2,1)S(1)}, bf16[96,1536]{1,0:T(8,128)(2,1)S(1)}, u32[]{:S(2)}, u32[]{:S(2)}) %collective-permute-start.46) | collective-permute-done | bytes 294944 | tf_op jit(solution)/shard_map/ppermute | solution.py:173
  90.2 4.3 %collective-permute-done.44.refs_0_ = bf16[96,1536]{1,0:T(8,128)(2,1)S(1)} collective-permute-done((bf16[96,1536]{1,0:T(8,128)(2,1)S(1)}, bf16[96,1536]{1,0:T(8,128)(2,1)S(1)}, u32[]{:S(2)}, u32[]{:S(2)}) %collective-permute-start.44) | collective-permute-done | bytes 294944 | tf_op jit(solution)/shard_map/ppermute | solution.py:173
  95.1 4.8 %shard_map.74 = (f32[768,1536]{1,0:T(8,128)}, f32[768,1536]{1,0:T(8,128)}, bf16[192,1536]{1,0:T(8,128)(2,1)S(1)}) custom-call(s32[4]{0:T(128)S(1)} %pad_add_fusion.s_ref.refs_0_, bf16[6144,1536]{1,0:T(8,128)(2,1)} %bitcast.30, bf16[768,1536]{1,0:T(8,128)(2,1)S(1)} %collective-permute-done.9.peer_ref.refs_2_, ...), custom_call_target="tpu_custom_call", output_to_operand_aliasing={{0}: (7, {}), {1}: (8, {})} | custom-call | tf_op jit(solution)/shard_map/pallas_call | solution.py:189
  99.9 4.8 %shard_map.75 = (f32[768,1536]{1,0:T(8,128)}, f32[768,1536]{1,0:T(8,128)}, bf16[192,1536]{1,0:T(8,128)(2,1)S(1)}) custom-call(s32[4]{0:T(128)S(1)} %pad_add_fusion.s_ref.refs_0_, bf16[6144,1536]{1,0:T(8,128)(2,1)} %bitcast.31, bf16[768,1536]{1,0:T(8,128)(2,1)S(1)} %collective-permute-done.6.peer_ref.refs_2_, ...), custom_call_target="tpu_custom_call", output_to_operand_aliasing={{0}: (7, {}), {1}: (8, {})} | custom-call | tf_op jit(solution)/shard_map/pallas_call | solution.py:189
  105.2 4.8 %shard_map.76 = (f32[768,1536]{1,0:T(8,128)}, f32[768,1536]{1,0:T(8,128)}, bf16[192,1536]{1,0:T(8,128)(2,1)S(1)}) custom-call(s32[4]{0:T(128)S(1)} %pad_add_fusion.s_ref.refs_0_, bf16[6144,1536]{1,0:T(8,128)(2,1)} %bitcast.32, bf16[768,1536]{1,0:T(8,128)(2,1)S(1)} %collective-permute-done.3.peer_ref.refs_2_, ...), custom_call_target="tpu_custom_call", output_to_operand_aliasing={{0}: (7, {}), {1}: (8, {})} | custom-call | tf_op jit(solution)/shard_map/pallas_call | solution.py:189
  112.1 4.1 %shard_map.77 = (f32[768,1536]{1,0:T(8,128)}, f32[768,1536]{1,0:T(8,128)}, bf16[96,1536]{1,0:T(8,128)(2,1)}) custom-call(s32[4]{0:T(128)S(1)} %pad_add_fusion.s_ref.refs_0_, bf16[6144,1536]{1,0:T(8,128)(2,1)} %bitcast.33, bf16[384,1536]{1,0:T(8,128)(2,1)S(1)} %collective-permute-done.peer_ref.refs_2_, ...), custom_call_target="tpu_custom_call", output_to_operand_aliasing={{0}: (7, {}), {1}: (8, {})} | custom-call | tf_op jit(solution)/shard_map/pallas_call | solution.py:189
  121.2 6.0 %collective-permute-done.15.refs_1_ = bf16[96,1536]{1,0:T(8,128)(2,1)} collective-permute-done((bf16[96,1536]{1,0:T(8,128)(2,1)}, bf16[96,1536]{1,0:T(8,128)(2,1)}, u32[]{:S(2)}, u32[]{:S(2)}) %collective-permute-start.15) | collective-permute-done | bytes 294944 | tf_op jit(solution)/shard_map/ppermute | solution.py:173
  128.5 9.0 %collective-permute-done.18.refs_2_ = bf16[96,1536]{1,0:T(8,128)(2,1)} collective-permute-done((bf16[96,1536]{1,0:T(8,128)(2,1)}, bf16[96,1536]{1,0:T(8,128)(2,1)}, u32[]{:S(2)}, u32[]{:S(2)}) %collective-permute-start.18) | collective-permute-done | bytes 294944 | tf_op jit(solution)/shard_map/ppermute | solution.py:173
  142.4 10.6 %collective-permute-done.32.refs_2_ = bf16[192,1536]{1,0:T(8,128)(2,1)S(1)} collective-permute-done((bf16[192,1536]{1,0:T(8,128)(2,1)S(1)}, bf16[192,1536]{1,0:T(8,128)(2,1)S(1)}, u32[]{:S(2)}, u32[]{:S(2)}) %collective-permute-start.32) | collective-permute-done | bytes 589856 | tf_op jit(solution)/shard_map/ppermute | solution.py:173
  156.9 3.2 %collective-permute-done.25.refs_2_ = bf16[192,1536]{1,0:T(8,128)(2,1)S(1)} collective-permute-done((bf16[192,1536]{1,0:T(8,128)(2,1)S(1)}, bf16[192,1536]{1,0:T(8,128)(2,1)S(1)}, u32[]{:S(2)}, u32[]{:S(2)}) %collective-permute-start.25) | collective-permute-done | bytes 589856 | tf_op jit(solution)/shard_map/ppermute | solution.py:173
  177.1 5.5 %collective-permute-done.23.refs_0_ = bf16[192,1536]{1,0:T(8,128)(2,1)} collective-permute-done((bf16[192,1536]{1,0:T(8,128)(2,1)S(1)}, bf16[192,1536]{1,0:T(8,128)(2,1)}, u32[]{:S(2)}, u32[]{:S(2)}) %collective-permute-start.23) | collective-permute-done | bytes 589856 | tf_op jit(solution)/shard_map/ppermute | solution.py:173
  196.2 2.4 %shard_map.80.refs_2_ = bf16[6144,1536]{1,0:T(8,128)(2,1)} custom-call(s32[6]{0:T(128)S(1)} %stack.47.s_ref, bf16[192,1536]{1,0:T(8,128)(2,1)S(1)} %get-tuple-element.31.refs_0_, bf16[192,1536]{1,0:T(8,128)(2,1)S(1)} %collective-permute-done.36.refs_1_, bf16[192,1536]{1,0:T(8,128)(2,1)S(1)} %collective-permute-done.39.refs_2_, ...), custom_call_target="tpu_custom_call", output_to_operand_aliasing={{}: (7, {})} | custom-call | tf_op jit(solution)/shard_map/pallas_call | solution.py:189
  200.5 2.4 %shard_map.82.refs_2_ = bf16[6144,1536]{1,0:T(8,128)(2,1)} custom-call(s32[6]{0:T(128)S(1)} %stack.47.s_ref, bf16[192,1536]{1,0:T(8,128)(2,1)S(1)} %get-tuple-element.30.refs_0_, bf16[192,1536]{1,0:T(8,128)(2,1)S(1)} %collective-permute-done.29.refs_1_, bf16[192,1536]{1,0:T(8,128)(2,1)S(1)} %copy-done.3, ...), custom_call_target="tpu_custom_call", output_to_operand_aliasing={{}: (7, {})} | custom-call | tf_op jit(solution)/shard_map/pallas_call | solution.py:189
  205.1 2.4 %shard_map.84.refs_2_ = bf16[6144,1536]{1,0:T(8,128)(2,1)} custom-call(s32[6]{0:T(128)S(1)} %stack.47.s_ref, bf16[192,1536]{1,0:T(8,128)(2,1)S(1)} %get-tuple-element.29.refs_0_, bf16[192,1536]{1,0:T(8,128)(2,1)S(1)} %copy-done.5, bf16[192,1536]{1,0:T(8,128)(2,1)S(1)} %copy-done.9, bf16[192,1536]{1,0:T(8,128)(2,1)S(1)} %copy-done.11, ...), custom_call_target="tpu_custom_call", output_to_operand_aliasing={{}: (7, {})} | custom-call | tf_op jit(solution)/shard_map/pallas_call | solution.py:189
  207.5 2.8 %shard_map.85.refs_6_ = bf16[6144,1536]{1,0:T(8,128)(2,1)} custom-call(s32[2]{0:T(128)S(1)} %pad_add_fusion.1.s_ref, bf16[192,1536]{1,0:T(8,128)(2,1)} %collective-permute-done.23.refs_0_, bf16[192,1536]{1,0:T(8,128)(2,1)} %collective-permute-done.24.refs_1_, bf16[6144,1536]{1,0:T(8,128)(2,1)} %shard_map.84.refs_2_), custom_call_target="tpu_custom_call", output_to_operand_aliasing={{}: (3, {})} | custom-call | tf_op jit(solution)/shard_map/pallas_call | solution.py:189
  210.4 3.2 %shard_map.86.refs_2_ = bf16[6144,1536]{1,0:T(8,128)(2,1)} custom-call(s32[6]{0:T(128)S(1)} %stack.47.s_ref, bf16[96,1536]{1,0:T(8,128)(2,1)} %get-tuple-element.28.refs_0_, bf16[96,1536]{1,0:T(8,128)(2,1)} %collective-permute-done.15.refs_1_, bf16[96,1536]{1,0:T(8,128)(2,1)} %collective-permute-done.18.refs_2_, ...), custom_call_target="tpu_custom_call", output_to_operand_aliasing={{}: (7, {})} | custom-call | tf_op jit(solution)/shard_map/pallas_call | solution.py:189
  213.6 2.4 %shard_map.87 = bf16[6144,1536]{1,0:T(8,128)(2,1)} custom-call(s32[2]{0:T(128)S(1)} %pad_add_fusion.1.s_ref, bf16[96,1536]{1,0:T(8,128)(2,1)} %collective-permute-done.16.refs_0_, bf16[96,1536]{1,0:T(8,128)(2,1)} %collective-permute-done.17.refs_1_, bf16[6144,1536]{1,0:T(8,128)(2,1)} %shard_map.86.refs_2_), custom_call_target="tpu_custom_call", output_to_operand_aliasing={{}: (3, {})} | custom-call | tf_op jit(solution)/shard_map/pallas_call | solution.py:189
  (205 shorter events, 93.6 us)
Async XLA Ops:
  12.2 42.1 %collective-permute-start = (bf16[384,1536]{1,0:T(8,128)(2,1)S(1)}, bf16[384,1536]{1,0:T(8,128)(2,1)S(1)}, u32[]{:S(2)}, u32[]{:S(2)}) collective-permute-start(bf16[384,1536]{1,0:T(8,128)(2,1)S(1)} %shard_map.58), channel_id=1, source_target_pairs={{0,4},{4,0},{8,12},{12,8},{16,20},{20,16},{24,28},{28,24},{1,5},{5... | collective-permute-start | bytes 3538952 | tf_op jit(solution)/shard_map/ppermute | solution.py:173
  14.8 52.8 %collective-permute-start.10 = (bf16[384,1536]{1,0:T(8,128)(2,1)S(1)}, bf16[384,1536]{1,0:T(8,128)(2,1)S(1)}, u32[]{:S(2)}, u32[]{:S(2)}) collective-permute-start(bf16[384,1536]{1,0:T(8,128)(2,1)S(1)} %shard_map.68), channel_id=1, source_target_pairs={{0,8},{4,20},{8,0},{12,28},{16,24},{20,4},{24,16},{28,12},{1,9},{5... | collective-permute-start | bytes 3538952 | tf_op jit(solution)/shard_map/ppermute | solution.py:173
  19.4 50.2 %collective-permute-start.7 = (bf16[384,1536]{1,0:T(8,128)(2,1)S(1)}, bf16[384,1536]{1,0:T(8,128)(2,1)S(1)}, u32[]{:S(2)}, u32[]{:S(2)}) collective-permute-start(bf16[384,1536]{1,0:T(8,128)(2,1)S(1)} %shard_map.65), channel_id=1, source_target_pairs={{0,8},{4,20},{8,0},{12,28},{16,24},{20,4},{24,16},{28,12},{1,9},{5... | collective-permute-start | bytes 3538952 | tf_op jit(solution)/shard_map/ppermute | solution.py:173
  21.2 29.3 %collective-permute-start.13 = (bf16[192,1536]{1,0:T(8,128)(2,1)S(1)}, bf16[192,1536]{1,0:T(8,128)(2,1)S(1)}, u32[]{:S(2)}, u32[]{:S(2)}) collective-permute-start(bf16[192,1536]{1,0:T(8,128)(2,1)S(1)} %shard_map.71), channel_id=1, source_target_pairs={{0,8},{4,20},{8,0},{12,28},{16,24},{20,4},{24,16},{28,12},{1,9},{5... | collective-permute-start | bytes 1769480 | tf_op jit(solution)/shard_map/ppermute | solution.py:173
  25.4 48.3 %collective-permute-start.4 = (bf16[384,1536]{1,0:T(8,128)(2,1)S(1)}, bf16[384,1536]{1,0:T(8,128)(2,1)S(1)}, u32[]{:S(2)}, u32[]{:S(2)}) collective-permute-start(bf16[384,1536]{1,0:T(8,128)(2,1)S(1)} %shard_map.62), channel_id=1, source_target_pairs={{0,8},{4,20},{8,0},{12,28},{16,24},{20,4},{24,16},{28,12},{1,9},{5... | collective-permute-start | bytes 3538952 | tf_op jit(solution)/shard_map/ppermute | solution.py:173
  56.0 22.0 %collective-permute-start.1 = (bf16[192,1536]{1,0:T(8,128)(2,1)S(1)}, bf16[192,1536]{1,0:T(8,128)(2,1)S(1)}, u32[]{:S(2)}, u32[]{:S(2)}) collective-permute-start(bf16[192,1536]{1,0:T(8,128)(2,1)S(1)} %shard_map.59), channel_id=1, source_target_pairs={{0,8},{4,20},{8,0},{12,28},{16,24},{20,4},{24,16},{28,12},{1,9},{5... | collective-permute-start | bytes 1769480 | tf_op jit(solution)/shard_map/ppermute | solution.py:173
  69.6 24.9 %collective-permute-start.11 = (bf16[192,1536]{1,0:T(8,128)(2,1)S(1)}, bf16[192,1536]{1,0:T(8,128)(2,1)S(1)}, u32[]{:S(2)}, u32[]{:S(2)}) collective-permute-start(bf16[192,1536]{1,0:T(8,128)(2,1)S(1)} %shard_map.69), channel_id=1, source_target_pairs={{0,16},{4,12},{8,24},{12,4},{16,0},{20,28},{24,8},{28,20},{1,17},{... | collective-permute-start | bytes 1769480 | tf_op jit(solution)/shard_map/ppermute | solution.py:173
  71.6 23.5 %collective-permute-start.8 = (bf16[192,1536]{1,0:T(8,128)(2,1)S(1)}, bf16[192,1536]{1,0:T(8,128)(2,1)S(1)}, u32[]{:S(2)}, u32[]{:S(2)}) collective-permute-start(bf16[192,1536]{1,0:T(8,128)(2,1)S(1)} %shard_map.66), channel_id=1, source_target_pairs={{0,16},{4,12},{8,24},{12,4},{16,0},{20,28},{24,8},{28,20},{1,17},{... | collective-permute-start | bytes 1769480 | tf_op jit(solution)/shard_map/ppermute | solution.py:173
  75.5 29.1 %collective-permute-start.5 = (bf16[192,1536]{1,0:T(8,128)(2,1)S(1)}, bf16[192,1536]{1,0:T(8,128)(2,1)S(1)}, u32[]{:S(2)}, u32[]{:S(2)}) collective-permute-start(bf16[192,1536]{1,0:T(8,128)(2,1)S(1)} %shard_map.63), channel_id=1, source_target_pairs={{0,16},{4,12},{8,24},{12,4},{16,0},{20,28},{24,8},{28,20},{1,17},{... | collective-permute-start | bytes 1769480 | tf_op jit(solution)/shard_map/ppermute | solution.py:173
  88.2 21.8 %collective-permute-start.2 = (bf16[96,1536]{1,0:T(8,128)(2,1)S(1)}, bf16[96,1536]{1,0:T(8,128)(2,1)S(1)}, u32[]{:S(2)}, u32[]{:S(2)}) collective-permute-start(bf16[96,1536]{1,0:T(8,128)(2,1)S(1)} %shard_map.60), channel_id=1, source_target_pairs={{0,16},{4,12},{8,24},{12,4},{16,0},{20,28},{24,8},{28,20},{1,17},{... | collective-permute-start | bytes 884744 | tf_op jit(solution)/shard_map/ppermute | solution.py:173
  94.5 21.7 %collective-permute-start.47 = (bf16[96,1536]{1,0:T(8,128)(2,1)S(1)}, bf16[96,1536]{1,0:T(8,128)(2,1)S(1)}, u32[]{:S(2)}, u32[]{:S(2)}) collective-permute-start(bf16[96,1536]{1,0:T(8,128)(2,1)S(1)} %get-tuple-element.32.refs_0_), channel_id=1, source_target_pairs={{0,4},{4,0},{8,12},{12,8},{16,20},{20,16},{24,28},{28,24},{1,5},{5... | collective-permute-start | bytes 884744 | tf_op jit(solution)/shard_map/ppermute | solution.py:173
  94.5 22.4 %collective-permute-start.48 = (bf16[96,1536]{1,0:T(8,128)(2,1)S(1)}, bf16[96,1536]{1,0:T(8,128)(2,1)S(1)}, u32[]{:S(2)}, u32[]{:S(2)}) collective-permute-start(bf16[96,1536]{1,0:T(8,128)(2,1)S(1)} %collective-permute-done.43.refs_1_), channel_id=1, source_target_pairs={{0,4},{4,0},{8,12},{12,8},{16,20},{20,16},{24,28},{28,24},{1,5},{5... | collective-permute-start | bytes 884744 | tf_op jit(solution)/shard_map/ppermute | solution.py:173
  95.0 24.6 %collective-permute-start.49 = (bf16[96,1536]{1,0:T(8,128)(2,1)S(1)}, bf16[96,1536]{1,0:T(8,128)(2,1)S(1)}, u32[]{:S(2)}, u32[]{:S(2)}) collective-permute-start(bf16[96,1536]{1,0:T(8,128)(2,1)S(1)} %collective-permute-done.46.refs_2_), channel_id=1, source_target_pairs={{0,4},{4,0},{8,12},{12,8},{16,20},{20,16},{24,28},{28,24},{1,5},{5... | collective-permute-start | bytes 884744 | tf_op jit(solution)/shard_map/ppermute | solution.py:173
  110.0 29.5 %collective-permute-start.36 = (bf16[192,1536]{1,0:T(8,128)(2,1)S(1)}, bf16[192,1536]{1,0:T(8,128)(2,1)S(1)}, u32[]{:S(2)}, u32[]{:S(2)}) collective-permute-start(bf16[192,1536]{1,0:T(8,128)(2,1)S(1)} %get-tuple-element.31.refs_0_), channel_id=1, source_target_pairs={{0,16},{4,12},{8,24},{12,4},{16,0},{20,28},{24,8},{28,20},{1,17},{... | collective-permute-start | bytes 1769480 | tf_op jit(solution)/shard_map/ppermute | solution.py:173
  117.7 21.8 %collective-permute-start.39 = (bf16[192,1536]{1,0:T(8,128)(2,1)S(1)}, bf16[192,1536]{1,0:T(8,128)(2,1)S(1)}, u32[]{:S(2)}, u32[]{:S(2)}) collective-permute-start(bf16[192,1536]{1,0:T(8,128)(2,1)S(1)} %get-tuple-element.31.refs_0_), channel_id=1, source_target_pairs={{0,8},{4,20},{8,0},{12,28},{16,24},{20,4},{24,16},{28,12},{1,9},{5... | collective-permute-start | bytes 1769480 | tf_op jit(solution)/shard_map/ppermute | solution.py:173
  120.4 17.1 %collective-permute-start.18 = (bf16[96,1536]{1,0:T(8,128)(2,1)}, bf16[96,1536]{1,0:T(8,128)(2,1)}, u32[]{:S(2)}, u32[]{:S(2)}) collective-permute-start(bf16[96,1536]{1,0:T(8,128)(2,1)} %get-tuple-element.28.refs_0_), channel_id=1, source_target_pairs={{0,8},{4,20},{8,0},{12,28},{16,24},{20,4},{24,16},{28,12},{1,9},{5... | collective-permute-start | bytes 884744 | tf_op jit(solution)/shard_map/ppermute | solution.py:173
  121.2 19.9 %collective-permute-start.40 = (bf16[192,1536]{1,0:T(8,128)(2,1)S(1)}, bf16[192,1536]{1,0:T(8,128)(2,1)S(1)}, u32[]{:S(2)}, u32[]{:S(2)}) collective-permute-start(bf16[192,1536]{1,0:T(8,128)(2,1)S(1)} %get-tuple-element.31.refs_0_), channel_id=1, source_target_pairs={{0,4},{4,0},{8,12},{12,8},{16,20},{20,16},{24,28},{28,24},{1,5},{5... | collective-permute-start | bytes 1769480 | tf_op jit(solution)/shard_map/ppermute | solution.py:173
  141.9 18.1 %collective-permute-start.25 = (bf16[192,1536]{1,0:T(8,128)(2,1)S(1)}, bf16[192,1536]{1,0:T(8,128)(2,1)S(1)}, u32[]{:S(2)}, u32[]{:S(2)}) collective-permute-start(bf16[192,1536]{1,0:T(8,128)(2,1)S(1)} %get-tuple-element.29.refs_0_), channel_id=1, source_target_pairs={{0,8},{4,20},{8,0},{12,28},{16,24},{20,4},{24,16},{28,12},{1,9},{5... | collective-permute-start | bytes 1769480 | tf_op jit(solution)/shard_map/ppermute | solution.py:173
  142.4 19.4 %collective-permute-start.26 = (bf16[192,1536]{1,0:T(8,128)(2,1)S(1)}, bf16[192,1536]{1,0:T(8,128)(2,1)S(1)}, u32[]{:S(2)}, u32[]{:S(2)}) collective-permute-start(bf16[192,1536]{1,0:T(8,128)(2,1)S(1)} %get-tuple-element.29.refs_0_), channel_id=1, source_target_pairs={{0,4},{4,0},{8,12},{12,8},{16,20},{20,16},{24,28},{28,24},{1,5},{5... | collective-permute-start | bytes 1769480 | tf_op jit(solution)/shard_map/ppermute | solution.py:173
  182.7 24.9 %collective-permute-start.24 = (bf16[192,1536]{1,0:T(8,128)(2,1)}, bf16[192,1536]{1,0:T(8,128)(2,1)}, u32[]{:S(2)}, u32[]{:S(2)}) collective-permute-start(bf16[192,1536]{1,0:T(8,128)(2,1)} %collective-permute-done.23.refs_0_), channel_id=1, source_target_pairs={{0,4},{4,0},{8,12},{12,8},{16,20},{20,16},{24,28},{28,24},{1,5},{5... | collective-permute-start | bytes 1769480 | tf_op jit(solution)/shard_map/ppermute | solution.py:173
  183.5 26.8 %collective-permute-start.19 = (bf16[96,1536]{1,0:T(8,128)(2,1)}, bf16[96,1536]{1,0:T(8,128)(2,1)}, u32[]{:S(2)}, u32[]{:S(2)}) collective-permute-start(bf16[96,1536]{1,0:T(8,128)(2,1)} %get-tuple-element.28.refs_0_), channel_id=1, source_target_pairs={{0,4},{4,0},{8,12},{12,8},{16,20},{20,16},{24,28},{28,24},{1,5},{5... | collective-permute-start | bytes 884744 | tf_op jit(solution)/shard_map/ppermute | solution.py:173
  184.8 25.5 %collective-permute-start.20 = (bf16[96,1536]{1,0:T(8,128)(2,1)}, bf16[96,1536]{1,0:T(8,128)(2,1)}, u32[]{:S(2)}, u32[]{:S(2)}) collective-permute-start(bf16[96,1536]{1,0:T(8,128)(2,1)} %collective-permute-done.15.refs_1_), channel_id=1, source_target_pairs={{0,4},{4,0},{8,12},{12,8},{16,20},{20,16},{24,28},{28,24},{1,5},{5... | collective-permute-start | bytes 884744 | tf_op jit(solution)/shard_map/ppermute | solution.py:173
  185.7 24.7 %collective-permute-start.21 = (bf16[96,1536]{1,0:T(8,128)(2,1)}, bf16[96,1536]{1,0:T(8,128)(2,1)}, u32[]{:S(2)}, u32[]{:S(2)}) collective-permute-start(bf16[96,1536]{1,0:T(8,128)(2,1)} %collective-permute-done.18.refs_2_), channel_id=1, source_target_pairs={{0,4},{4,0},{8,12},{12,8},{16,20},{20,16},{24,28},{28,24},{1,5},{5... | collective-permute-start | bytes 884744 | tf_op jit(solution)/shard_map/ppermute | solution.py:173
  187.0 26.6 %collective-permute-start.17 = (bf16[96,1536]{1,0:T(8,128)(2,1)}, bf16[96,1536]{1,0:T(8,128)(2,1)}, u32[]{:S(2)}, u32[]{:S(2)}) collective-permute-start(bf16[96,1536]{1,0:T(8,128)(2,1)} %collective-permute-done.16.refs_0_), channel_id=1, source_target_pairs={{0,4},{4,0},{8,12},{12,8},{16,20},{20,16},{24,28},{28,24},{1,5},{5... | collective-permute-start | bytes 884744 | tf_op jit(solution)/shard_map/ppermute | solution.py:173
  (74 other events, 433.6 us)

commit v2 on v0

v2 whole, which is shorter than its diff:
```python
import functools
import string

import jax
import jax.numpy as jnp
from jax import lax
from jax.experimental import pallas as pl
from jax.experimental.pallas import tpu as pltpu
from jax.sharding import PartitionSpec as P


beta_one = 0.9
beta_two = 0.99
step_size = 0.1
decay_rate = 0.1
softness = 0.05

UNITS = 16
CHUNKS = (2, 3, 4, 4, 2, 1)
ORDER = (
    "ld0", "d0", "ld1", "d1", "comb0", "R0", "ld2", "comb1", "d2", "R1", "sec0", "r0", "ld3", "comb2", "R2",
    "sec1", "r1", "ld4", "d4", "upd0", "b0", "d3", "ld6", "a0", "upd1", "ld5", "comb4", "R4", "d5", "comb5",
    "R5", "comb3", "R3", "st0", "o0", "f0", "sec4", "r4", "upd4", "sec5", "r5", "ld7", "upd5", "a5", "A0",
    "b5", "a1", "st5", "sec2", "A5", "r2", "o4", "sec3", "r3", "f5", "B0", "upd2", "a2", "o5", "F5", "pf5",
    "a4", "upd3", "o3", "a3", "pa0", "st3", "A1", "b4", "b1", "f1", "st4", "o1", "A2", "b3", "st2", "A4",
    "B4", "f4", "B5", "pa5", "b2", "f2", "pa4", "A3", "F1", "pf1", "B3", "o2", "f3", "F0", "B1", "pa1", "F4",
    "pf0", "B2", "pa3", "pa2", "F2", "st1", "pf2", "F3", "pf4", "pf3",
)
MOVES = {
    "d": ("cut", "across"),
    "R": ("comb", "first"),
    "r": ("sec", "second"),
    "a": ("upd", "second"),
    "b": ("upd", "first"),
    "o": ("upd", "across"),
    "f": ("a", "first"),
    "A": ("a", "across"),
    "B": ("b", "across"),
    "F": ("f", "across"),
}
SOURCES = {"pa": ("upd", "a", "b", "o", "A", "B"), "pf": ("f", "F")}
PLACED = {"pa": ((0, 0), (2, 0), (1, 0), (0, 1), (1, 1), (2, 1)), "pf": ((3, 0), (3, 1))}
ROWS = 16
VMEM_LIMIT = 4 << 20


def lion_update(gradient, master, momentum):
    interp = beta_one * momentum + (1.0 - beta_one) * gradient
    direction = interp * lax.rsqrt(interp * interp + softness * softness)
    new_master = master - step_size * (direction + decay_rate * master)
    new_momentum = beta_two * momentum + (1.0 - beta_two) * gradient
    return (new_master, new_momentum)


def per_device_collectives(grad_parts, master, momentum):
    replicas = lax.axis_size("dp")
    summed = lax.psum_scatter(grad_parts[0], "dp", scatter_dimension=1, tiled=True)
    gradient = summed.astype(jnp.float32) / replicas
    new_master, new_momentum = lion_update(gradient, master, momentum)
    new_weights = lax.all_gather(new_master.astype(jnp.bfloat16), "dp", axis=1, tiled=True)
    return (new_master, new_momentum, new_weights)


def rows_loop(rows, body):
    @pl.loop(0, rows // ROWS)
    def _(i):
        body(pl.multiple_of(i * ROWS, ROWS))


def at(ref, row, rows=ROWS):
    return ref.at[pl.ds(row, rows), :]


def f32(ref, row):
    return ref[pl.ds(row, ROWS), :].astype(jnp.float32)


def run_copies(pairs, sem):
    copies = [pltpu.make_async_copy(src, dst, sem.at[i]) for i, (src, dst) in enumerate(pairs)]
    for c in copies:
        c.start()
    for c in copies:
        c.wait()


def load_kernel(jobs, tile, s_ref, grad_ref, master_ref, momentum_ref, *rest):
    outs, sem = list(rest[:-1]), rest[-1]
    pairs = []
    for kind, rows, row0 in jobs:
        if kind == "mm":
            for src in (master_ref, momentum_ref):
                pairs.append((at(src, row0, rows), outs.pop(0)))
        else:
            core = s_ref[0] % 2
            held = core if kind == "own" else 1 - core
            dst = outs.pop(0)
            for m in range(4):
                pairs.append((at(grad_ref, (2 * m + held) * tile + row0, rows), at(dst, m * rows, rows)))
    run_copies(pairs, sem)


def combine_kernel(rows, s_ref, own_ref, peer_ref, out_ref):
    for j in range(2):
        base = (s_ref[1 + 2 * j] // 2) * rows

        def body(row):
            total = f32(own_ref, base + row) + f32(peer_ref, base + row)
            out_ref[pl.ds(j * rows + row, ROWS), :] = total.astype(jnp.bfloat16)

        rows_loop(rows, body)


def second_kernel(rows, s_ref, own_ref, peer_ref, recv_ref, out_ref):
    base = (s_ref[2] // 2) * rows

    def body(row):
        total = f32(own_ref, base + row) + f32(peer_ref, base + row) + f32(recv_ref, rows + row)
        out_ref[pl.ds(row, ROWS), :] = total.astype(jnp.bfloat16)

    rows_loop(rows, body)


def update_kernel(rows, scale, s_ref, own_ref, peer_ref, first_ref, second_ref, master_ref, momentum_ref, *outs):
    new_master_ref, new_momentum_ref, weights_ref = outs
    base = (s_ref[0] // 2) * rows

    def body(row):
        summed = (f32(own_ref, base + row) + f32(peer_ref, base + row)) + (f32(first_ref, row) + f32(second_ref, row))
        here = pl.ds(row, ROWS)
        new_master, new_momentum = lion_update(summed * scale, master_ref[here, :], momentum_ref[here, :])
        new_master_ref[here, :] = new_master
        new_momentum_ref[here, :] = new_momentum
        weights_ref[here, :] = new_master.astype(jnp.bfloat16)

    rows_loop(rows, body)


def place_kernel(which, rows, row0, tile, s_ref, *refs):
    out_ref, sem = refs[-2:]
    pairs = []
    for src, (i, other) in zip(refs, which):
        pairs.append((src, at(out_ref, (s_ref[i] ^ other) * tile + row0, rows)))
    run_copies(pairs, sem)


def store_kernel(rows, row0, s_ref, master_ref, momentum_ref, *rest):
    new_master_ref, new_momentum_ref, sem = rest[-3:]
    run_copies([(master_ref, at(new_master_ref, row0, rows)), (momentum_ref, at(new_momentum_ref, row0, rows))], sem)


def per_device(grad_parts, master, momentum):
    replicas = lax.axis_size("dp")
    _, _, total_rows, cols = grad_parts.shape
    tile = total_rows // replicas
    if replicas != 8 or tile % (UNITS * ROWS):
        return per_device_collectives(grad_parts, master, momentum)
    bf = jnp.bfloat16
    sizes = [n * (tile // UNITS) for n in CHUNKS]
    starts = [sum(sizes[:k]) for k in range(len(sizes))]

    grad = grad_parts.reshape(total_rows, cols)
    master = master.reshape(tile, cols)
    momentum = momentum.reshape(tile, cols)
    me = lax.axis_index("dp")
    first = jnp.where(me & 1 == 0, 2, 4)
    second = 6 - first
    scal = jnp.stack([me, me ^ first, me ^ second, me ^ 6]).astype(jnp.int32)

    def first_bit(i):
        return 4 if i & 1 else 2

    perms = {
        "first": [(i, i ^ first_bit(i)) for i in range(replicas)],
        "second": [(i, i ^ 6 ^ first_bit(i)) for i in range(replicas)],
        "across": [(i, i ^ 1) for i in range(replicas)],
    }

    def near(rows, dtype=bf):
        return pltpu.VMEM((rows, cols), dtype)

    def call(kernel, tiles, far, close, outs, copies=0, aliases=None):
        spaces = [pltpu.HBM] * len(far) + [pltpu.VMEM] * len(close)
        args = [pltpu.with_memory_space_constraint(x, space) for x, space in zip([*far, *close], spaces)]
        return pl.pallas_call(
            kernel,
            grid_spec=pltpu.PrefetchScalarGridSpec(
                num_scalar_prefetch=1,
                grid=(),
                in_specs=[pl.BlockSpec(memory_space=space) for space in spaces],
                out_specs=[pl.BlockSpec(memory_space=o.memory_space) for o in outs],
                scratch_shapes=[pltpu.SemaphoreType.DMA((copies,))] if copies else [],
            ),
            out_shape=outs,
            input_output_aliases=aliases or {},
            compiler_params=pltpu.CompilerParams(vmem_limit_bytes=VMEM_LIMIT),
        )(tiles, *args)

    def load(names):
        jobs, outs, copies = [], [], 0
        for kind, k in names:
            jobs.append((kind, sizes[k], starts[k]))
            outs += [near(sizes[k], jnp.float32)] * 2 if kind == "mm" else [near(4 * sizes[k])]
            copies += 2 if kind == "mm" else 4
        kernel = functools.partial(load_kernel, jobs, tile)
        got = list(call(kernel, scal, [grad, master, momentum], [], outs, copies))
        for kind, k in names:
            held[kind, k] = [got.pop(0), got.pop(0)] if kind == "mm" else got.pop(0)

    def write(kernel, sources, shapes, finals):
        n = len(finals)
        body = lambda s_ref, *refs: kernel(s_ref, *refs[n:])
        got = call(body, scal, finals, sources, shapes, len(sources), {1 + i: i for i in range(n)})
        finals[:] = got

    weights_shape = [pltpu.HBM((total_rows, cols), bf)]
    state_shape = [pltpu.HBM((tile, cols), jnp.float32)] * 2
    held, weights, state, last = {}, [], [], len(CHUNKS)
    for name in ORDER:
        kind, k = name.rstrip(string.digits), int(name.lstrip(string.ascii_letters))
        rows = sizes[k] if k < last else 0
        get = lambda *kinds: [held[kind, k] for kind in kinds]
        if kind in MOVES:
            source, how = MOVES[kind]
            held[kind, k] = lax.ppermute(held[source, k], "dp", perms[how])
        elif kind == "ld":
            load([(what, k - i) for i, what in enumerate(("cut", "own", "mm")) if 0 <= k - i < last])
        elif kind == "comb":
            kernel = functools.partial(combine_kernel, rows)
            (held[kind, k],) = call(kernel, scal, [], get("own", "d"), [near(2 * rows)])
        elif kind == "sec":
            kernel = functools.partial(second_kernel, rows)
            (held[kind, k],) = call(kernel, scal, [], get("own", "d", "R"), [near(rows)])
        elif kind == "upd":
            kernel = functools.partial(update_kernel, rows, 1.0 / replicas)
            outs = [near(rows, jnp.float32), near(rows, jnp.float32), near(rows)]
            args = get("own", "d", "R", "r") + held["mm", k]
            *held["new", k], held[kind, k] = call(kernel, scal, [], args, outs, 0, {5: 0, 6: 1})
        elif kind == "st":
            kernel = functools.partial(store_kernel, rows, starts[k])
            write(kernel, held["new", k], state_shape, state)
        else:
            kernel = functools.partial(place_kernel, PLACED[kind], rows, starts[k], tile)
            write(kernel, get(*SOURCES[kind]), weights_shape, weights)
    shape = (1, tile, cols)
    return (state[0].reshape(shape), state[1].reshape(shape), weights[0].reshape(1, total_rows, cols))


def solution(mesh):
    return jax.shard_map(
        per_device,
        mesh=mesh,
        in_specs=(P("dp", None, None, "mp"), P(None, "dp", "mp"), P(None, "dp", "mp")),
        out_specs=(P(None, "dp", "mp"), P(None, "dp", "mp"), P(None, None, "mp")),
        check_vma=False,
    )
```

time: 272 us -> 232 us (0.85)
  waiting for transfers between devices: 232 us -> 123 us
  Pallas kernels: 0 us -> 68.9 us
  starting transfers between devices: 0.08 us -> 38.8 us
  local copies, waits for them, and re-layouts: 16.5 us -> 0 us
  between operations: 14 us -> 1.17 us
  other arithmetic: 8.67 us -> 0.08 us
    reduce_scatter x1 -> x0, waiting for transfers between devices: 133 us -> none  [per_device(): lax.psum_scatter(partials.astype(jnp.bfloat16), 'dp', scatter_dimension=1...]
    ppermute x0 -> x60, waiting for transfers between devices: none -> 123 us  [per_device(): held[kind, k] = lax.ppermute(held[source, k], 'dp', perms[how])]
    all_gather x1 -> x0, waiting for transfers between devices: 98.7 us -> none  [per_device(): lax.all_gather(new_master.astype(jnp.bfloat16), 'dp', axis=1, tiled=True)]
    pallas_call x0 -> x44, Pallas kernels: none -> 68.9 us  [call(): pl.pallas_call(kernel, grid_spec=pltpu.PrefetchScalarGridSpec(num_scalar_...]
    ppermute x0 -> x60, starting transfers between devices: none -> 38.8 us  [per_device(): held[kind, k] = lax.ppermute(held[source, k], 'dp', perms[how])]
    unnamed x1 -> x0, local copies, waits for them, and re-layouts: 16.5 us -> none
    convert_element_type x1 -> x0, other arithmetic: 8.67 us -> none  [per_device(): new_master.astype(jnp.bfloat16)]
  transfers between devices with their start and end apart: 2 -> 60, of which waited for: 2 -> 18; matrix products, arithmetic and copies ran while one was open for 0% -> 0% of each run, Pallas kernels for 0% -> 27%
where the time goes in v2:
time: 232 us
  waiting for transfers between devices  123 us (53%)
  Pallas kernels  68.9 us (30%)
  starting transfers between devices  38.8 us (17%)
    ppermute x60, waiting for transfers between devices, per_device(): held[kind, k] = lax.ppermute(held[source, k], 'dp', perms[how])  123 us
    pallas_call x44, Pallas kernels, call(): pl.pallas_call(kernel, grid_spec=pltpu.PrefetchScalarGridSpec(num_scalar_...  68.9 us
    ppermute x60, starting transfers between devices, per_device(): held[kind, k] = lax.ppermute(held[source, k], 'dp', perms[how])  38.8 us
  transfers between devices with their start and end apart: 60, of which 18 were waited for; matrix products, arithmetic and copies ran while one was open for 0% of the time, Pallas kernels for 27%

profile of v2, /device:TPU:0, one launch (start us, length us, event | category | flops | bytes accessed | tf_op | source)
XLA Modules:
  0.0 231.9 jit_solution(17816243825662712958)
XLA Ops:
  0.7 2.9 %shard_map.66 = (bf16[192,1536]{1,0:T(8,128)(2,1)S(1)}, bf16[384,1536]{1,0:T(8,128)(2,1)S(1)}, f32[192,1536]{1,0:T(8,128)S(1)}, f32[192,1536]{1,0:T(8,128)S(1)}) custom-call(s32[4]{0:T(128)S(1)} %pad_add_fusion.s_ref, bf16[6144,1536]{1,0:T(8,128)(2,1)} %bitcast.11, f32[768,1536]{1,0:T(8,128)} %bitcast.19, f32[768,1536]{1,0:T(8,128)} %bitcast.27), custom_call_target="tpu_custom_call" | custom-call | tf_op jit(solution)/shard_map/pallas_call | solution.py:184
  4.2 2.1 shard_map.65
  7.0 2.6 %collective-permute-start.4 = (bf16[96,1536]{1,0:T(8,128)(2,1)S(1)}, bf16[96,1536]{1,0:T(8,128)(2,1)S(1)}, u32[]{:S(2)}, u32[]{:S(2)}) collective-permute-start(bf16[96,1536]{1,0:T(8,128)(2,1)S(1)} %shard_map.67), channel_id=1, source_target_pairs={{0,8},{4,20},{8,0},{12,28},{16,24},{20,4},{24,16},{28,12},{1,9},{5... | collective-permute-start | bytes 884744 | tf_op jit(solution)/shard_map/ppermute | solution.py:224
  9.6 2.4 %shard_map.58 = (bf16[576,1536]{1,0:T(8,128)(2,1)S(1)}, bf16[384,1536]{1,0:T(8,128)(2,1)S(1)}) custom-call(s32[4]{0:T(128)S(1)} %pad_add_fusion.s_ref, bf16[6144,1536]{1,0:T(8,128)(2,1)} %bitcast.13, f32[768,1536]{1,0:T(8,128)} %bitcast.21, f32[768,1536]{1,0:T(8,128)} %bitcast.29), custom_call_target="tpu_custom_call" | custom-call | tf_op jit(solution)/shard_map/pallas_call | solution.py:184
  17.0 3.5 %shard_map.73 = (bf16[768,1536]{1,0:T(8,128)(2,1)S(1)}, bf16[768,1536]{1,0:T(8,128)(2,1)S(1)}, f32[144,1536]{1,0:T(8,128)S(1)}, f32[144,1536]{1,0:T(8,128)S(1)}) custom-call(s32[4]{0:T(128)S(1)} %pad_add_fusion.s_ref, bf16[6144,1536]{1,0:T(8,128)(2,1)} %bitcast.15, f32[768,1536]{1,0:T(8,128)} %bitcast.23, f32[768,1536]{1,0:T(8,128)} %bitcast.31), custom_call_target="tpu_custom_call" | custom-call | tf_op jit(solution)/shard_map/pallas_call | solution.py:184
  20.6 3.1 %shard_map.62 = (bf16[768,1536]{1,0:T(8,128)(2,1)S(1)}, bf16[576,1536]{1,0:T(8,128)(2,1)S(1)}, f32[96,1536]{1,0:T(8,128)S(1)}, f32[96,1536]{1,0:T(8,128)S(1)}) custom-call(s32[4]{0:T(128)S(1)} %pad_add_fusion.s_ref, bf16[6144,1536]{1,0:T(8,128)(2,1)} %bitcast.16, f32[768,1536]{1,0:T(8,128)} %bitcast.24, f32[768,1536]{1,0:T(8,128)} %bitcast.32), custom_call_target="tpu_custom_call" | custom-call | tf_op jit(solution)/shard_map/pallas_call | solution.py:184
  27.2 3.3 %shard_map.72 = (bf16[384,1536]{1,0:T(8,128)(2,1)S(1)}, bf16[768,1536]{1,0:T(8,128)(2,1)S(1)}, f32[192,1536]{1,0:T(8,128)S(1)}, f32[192,1536]{1,0:T(8,128)S(1)}) custom-call(s32[4]{0:T(128)S(1)} %pad_add_fusion.s_ref, bf16[6144,1536]{1,0:T(8,128)(2,1)} %bitcast.18, f32[768,1536]{1,0:T(8,128)} %bitcast.26, f32[768,1536]{1,0:T(8,128)} %bitcast.34), custom_call_target="tpu_custom_call" | custom-call | tf_op jit(solution)/shard_map/pallas_call | solution.py:184
  34.3 2.9 %collective-permute-done.26.refs_3_ = bf16[48,1536]{1,0:T(8,128)(2,1)S(1)} collective-permute-done((bf16[48,1536]{1,0:T(8,128)(2,1)S(1)}, bf16[48,1536]{1,0:T(8,128)(2,1)S(1)}, u32[]{:S(2)}, u32[]{:S(2)}) %collective-permute-start.26) | collective-permute-done | bytes 147488 | tf_op jit(solution)/shard_map/ppermute | solution.py:224
  42.5 6.1 %collective-permute-done.19.refs_0_ = bf16[48,1536]{1,0:T(8,128)(2,1)S(1)} collective-permute-done((bf16[48,1536]{1,0:T(8,128)(2,1)S(1)}, bf16[48,1536]{1,0:T(8,128)(2,1)S(1)}, u32[]{:S(2)}, u32[]{:S(2)}) %collective-permute-start.19) | collective-permute-done | bytes 147488 | tf_op jit(solution)/shard_map/ppermute | solution.py:224
  52.0 3.7 %collective-permute-done.10.recv_ref.first_ref = bf16[192,1536]{1,0:T(8,128)(2,1)S(1)} collective-permute-done((bf16[192,1536]{1,0:T(8,128)(2,1)S(1)}, bf16[192,1536]{1,0:T(8,128)(2,1)S(1)}, u32[]{:S(2)}, u32[]{:S(2)}) %collective-permute-start.10) | collective-permute-done | bytes 589856 | tf_op jit(solution)/shard_map/ppermute | solution.py:224
  55.6 5.7 %collective-permute-done.2.second_ref = bf16[96,1536]{1,0:T(8,128)(2,1)S(1)} collective-permute-done((bf16[96,1536]{1,0:T(8,128)(2,1)S(1)}, bf16[96,1536]{1,0:T(8,128)(2,1)S(1)}, u32[]{:S(2)}, u32[]{:S(2)}) %collective-permute-start.2) | collective-permute-done | bytes 294944 | tf_op jit(solution)/shard_map/ppermute | solution.py:224
  73.4 5.0 %collective-permute-done.21.refs_2_ = bf16[96,1536]{1,0:T(8,128)(2,1)S(1)} collective-permute-done((bf16[96,1536]{1,0:T(8,128)(2,1)S(1)}, bf16[96,1536]{1,0:T(8,128)(2,1)S(1)}, u32[]{:S(2)}, u32[]{:S(2)}) %collective-permute-start.21) | collective-permute-done | bytes 294944 | tf_op jit(solution)/shard_map/ppermute | solution.py:224
  83.0 14.8 %collective-permute-done.30.refs_2_ = bf16[96,1536]{1,0:T(8,128)(2,1)S(1)} collective-permute-done((bf16[96,1536]{1,0:T(8,128)(2,1)S(1)}, bf16[96,1536]{1,0:T(8,128)(2,1)S(1)}, u32[]{:S(2)}, u32[]{:S(2)}) %collective-permute-start.30) | collective-permute-done | bytes 294944 | tf_op jit(solution)/shard_map/ppermute | solution.py:224
  97.8 15.6 %collective-permute-done.31.refs_3_ = bf16[96,1536]{1,0:T(8,128)(2,1)S(1)} collective-permute-done((bf16[96,1536]{1,0:T(8,128)(2,1)S(1)}, bf16[96,1536]{1,0:T(8,128)(2,1)S(1)}, u32[]{:S(2)}, u32[]{:S(2)}) %collective-permute-start.31) | collective-permute-done | bytes 294944 | tf_op jit(solution)/shard_map/ppermute | solution.py:224
  120.9 6.8 %collective-permute-done.35.refs_2_ = bf16[144,1536]{1,0:T(8,128)(2,1)S(1)} collective-permute-done((bf16[144,1536]{1,0:T(8,128)(2,1)S(1)}, bf16[144,1536]{1,0:T(8,128)(2,1)S(1)}, u32[]{:S(2)}, u32[]{:S(2)}) %collective-permute-start.35) | collective-permute-done | bytes 442400 | tf_op jit(solution)/shard_map/ppermute | solution.py:224
  127.7 2.1 collective-permute-start.36
  130.7 20.4 %collective-permute-done.56.refs_1_ = bf16[96,1536]{1,0:T(8,128)(2,1)S(1)} collective-permute-done((bf16[96,1536]{1,0:T(8,128)(2,1)S(1)}, bf16[96,1536]{1,0:T(8,128)(2,1)S(1)}, u32[]{:S(2)}, u32[]{:S(2)}) %collective-permute-start.56) | collective-permute-done | bytes 294944 | tf_op jit(solution)/shard_map/ppermute | solution.py:224
  160.0 11.6 %collective-permute-done.44.refs_2_ = bf16[192,1536]{1,0:T(8,128)(2,1)S(1)} collective-permute-done((bf16[192,1536]{1,0:T(8,128)(2,1)S(1)}, bf16[192,1536]{1,0:T(8,128)(2,1)S(1)}, u32[]{:S(2)}, u32[]{:S(2)}) %collective-permute-start.44) | collective-permute-done | bytes 589856 | tf_op jit(solution)/shard_map/ppermute | solution.py:224
  173.0 11.3 %collective-permute-done.49.refs_2_ = bf16[192,1536]{1,0:T(8,128)(2,1)S(1)} collective-permute-done((bf16[192,1536]{1,0:T(8,128)(2,1)S(1)}, bf16[192,1536]{1,0:T(8,128)(2,1)S(1)}, u32[]{:S(2)}, u32[]{:S(2)}) %collective-permute-start.49) | collective-permute-done | bytes 589856 | tf_op jit(solution)/shard_map/ppermute | solution.py:224
  186.8 7.3 %collective-permute-done.54.refs_1_ = bf16[192,1536]{1,0:T(8,128)(2,1)S(1)} collective-permute-done((bf16[192,1536]{1,0:T(8,128)(2,1)S(1)}, bf16[192,1536]{1,0:T(8,128)(2,1)S(1)}, u32[]{:S(2)}, u32[]{:S(2)}) %collective-permute-start.54) | collective-permute-done | bytes 589856 | tf_op jit(solution)/shard_map/ppermute | solution.py:224
  194.1 6.3 %collective-permute-done.58.refs_1_ = bf16[192,1536]{1,0:T(8,128)(2,1)S(1)} collective-permute-done((bf16[192,1536]{1,0:T(8,128)(2,1)S(1)}, bf16[192,1536]{1,0:T(8,128)(2,1)S(1)}, u32[]{:S(2)}, u32[]{:S(2)}) %collective-permute-start.58) | collective-permute-done | bytes 589856 | tf_op jit(solution)/shard_map/ppermute | solution.py:224
  219.1 2.1 shard_map.95.refs_0_
  222.6 2.4 %shard_map.97.refs_0_ = bf16[6144,1536]{1,0:T(8,128)(2,1)} custom-call(s32[4]{0:T(128)S(1)} %pad_add_fusion.s_ref, bf16[6144,1536]{1,0:T(8,128)(2,1)} %shard_map.96.refs_0_, bf16[192,1536]{1,0:T(8,128)(2,1)S(1)} %get-tuple-element.107.refs_1_, bf16[192,1536]{1,0:T(8,128)(2,1)S(1)} %collective-permute-done.44.refs_2_, ...), custom_call_target="tpu_custom_call", output_to_operand_aliasing={{}: (1, {})} | custom-call | tf_op jit(solution)/shard_map/pallas_call | solution.py:184
  225.0 2.4 %shard_map.98.refs_0_ = bf16[6144,1536]{1,0:T(8,128)(2,1)} custom-call(s32[4]{0:T(128)S(1)} %pad_add_fusion.s_ref, bf16[6144,1536]{1,0:T(8,128)(2,1)} %shard_map.97.refs_0_, bf16[192,1536]{1,0:T(8,128)(2,1)S(1)} %get-tuple-element.108.refs_1_, bf16[192,1536]{1,0:T(8,128)(2,1)S(1)} %collective-permute-done.49.refs_2_, ...), custom_call_target="tpu_custom_call", output_to_operand_aliasing={{}: (1, {})} | custom-call | tf_op jit(solution)/shard_map/pallas_call | solution.py:184
  (141 shorter events, 84.4 us)
Async XLA Ops:
  12.0 26.7 %collective-permute-start.15 = (bf16[576,1536]{1,0:T(8,128)(2,1)S(1)}, bf16[576,1536]{1,0:T(8,128)(2,1)S(1)}, u32[]{:S(2)}, u32[]{:S(2)}) collective-permute-start(bf16[576,1536]{1,0:T(8,128)(2,1)S(1)} %get-tuple-element.96), channel_id=1, source_target_pairs={{0,4},{4,0},{8,12},{12,8},{16,20},{20,16},{24,28},{28,24},{1,5},{5... | collective-permute-start | bytes 5308424 | tf_op jit(solution)/shard_map/ppermute | solution.py:224
  14.1 17.9 %collective-permute-start = (bf16[384,1536]{1,0:T(8,128)(2,1)S(1)}, bf16[384,1536]{1,0:T(8,128)(2,1)S(1)}, u32[]{:S(2)}, u32[]{:S(2)}) collective-permute-start(bf16[384,1536]{1,0:T(8,128)(2,1)S(1)} %shard_map.59), channel_id=1, source_target_pairs={{0,4},{4,0},{8,12},{12,8},{16,20},{20,16},{24,28},{28,24},{1,5},{5... | collective-permute-start | bytes 3538952 | tf_op jit(solution)/shard_map/ppermute | solution.py:224
  20.6 44.7 %collective-permute-start.6 = (bf16[768,1536]{1,0:T(8,128)(2,1)S(1)}, bf16[768,1536]{1,0:T(8,128)(2,1)S(1)}, u32[]{:S(2)}, u32[]{:S(2)}) collective-permute-start(bf16[768,1536]{1,0:T(8,128)(2,1)S(1)} %get-tuple-element.72), channel_id=1, source_target_pairs={{0,4},{4,0},{8,12},{12,8},{16,20},{20,16},{24,28},{28,24},{1,5},{5... | collective-permute-start | bytes 7077896 | tf_op jit(solution)/shard_map/ppermute | solution.py:224
  23.8 43.0 %collective-permute-start.12 = (bf16[768,1536]{1,0:T(8,128)(2,1)S(1)}, bf16[768,1536]{1,0:T(8,128)(2,1)S(1)}, u32[]{:S(2)}, u32[]{:S(2)}) collective-permute-start(bf16[768,1536]{1,0:T(8,128)(2,1)S(1)} %get-tuple-element.88), channel_id=1, source_target_pairs={{0,4},{4,0},{8,12},{12,8},{16,20},{20,16},{24,28},{28,24},{1,5},{5... | collective-permute-start | bytes 7077896 | tf_op jit(solution)/shard_map/ppermute | solution.py:224
  48.6 20.2 %collective-permute-start.16 = (bf16[288,1536]{1,0:T(8,128)(2,1)S(1)}, bf16[288,1536]{1,0:T(8,128)(2,1)S(1)}, u32[]{:S(2)}, u32[]{:S(2)}) collective-permute-start(bf16[288,1536]{1,0:T(8,128)(2,1)S(1)} %shard_map.86), channel_id=1, source_target_pairs={{0,8},{4,20},{8,0},{12,28},{16,24},{20,4},{24,16},{28,12},{1,9},{5... | collective-permute-start | bytes 2654216 | tf_op jit(solution)/shard_map/ppermute | solution.py:224
  66.8 49.8 %collective-permute-start.7 = (bf16[384,1536]{1,0:T(8,128)(2,1)S(1)}, bf16[384,1536]{1,0:T(8,128)(2,1)S(1)}, u32[]{:S(2)}, u32[]{:S(2)}) collective-permute-start(bf16[384,1536]{1,0:T(8,128)(2,1)S(1)} %shard_map.74), channel_id=1, source_target_pairs={{0,8},{4,20},{8,0},{12,28},{16,24},{20,4},{24,16},{28,12},{1,9},{5... | collective-permute-start | bytes 3538952 | tf_op jit(solution)/shard_map/ppermute | solution.py:224
  72.1 57.7 %collective-permute-start.13 = (bf16[384,1536]{1,0:T(8,128)(2,1)S(1)}, bf16[384,1536]{1,0:T(8,128)(2,1)S(1)}, u32[]{:S(2)}, u32[]{:S(2)}) collective-permute-start(bf16[384,1536]{1,0:T(8,128)(2,1)S(1)} %shard_map.82), channel_id=1, source_target_pairs={{0,8},{4,20},{8,0},{12,28},{16,24},{20,4},{24,16},{28,12},{1,9},{5... | collective-permute-start | bytes 3538952 | tf_op jit(solution)/shard_map/ppermute | solution.py:224
  78.5 35.0 %collective-permute-start.17 = (bf16[144,1536]{1,0:T(8,128)(2,1)S(1)}, bf16[144,1536]{1,0:T(8,128)(2,1)S(1)}, u32[]{:S(2)}, u32[]{:S(2)}) collective-permute-start(bf16[144,1536]{1,0:T(8,128)(2,1)S(1)} %shard_map.87), channel_id=1, source_target_pairs={{0,16},{4,12},{8,24},{12,4},{16,0},{20,28},{24,8},{28,20},{1,17},{... | collective-permute-start | bytes 1327112 | tf_op jit(solution)/shard_map/ppermute | solution.py:224
  80.1 17.7 %collective-permute-start.30 = (bf16[96,1536]{1,0:T(8,128)(2,1)S(1)}, bf16[96,1536]{1,0:T(8,128)(2,1)S(1)}, u32[]{:S(2)}, u32[]{:S(2)}) collective-permute-start(bf16[96,1536]{1,0:T(8,128)(2,1)S(1)} %get-tuple-element.105.refs_1_), channel_id=1, source_target_pairs={{0,16},{4,12},{8,24},{12,4},{16,0},{20,28},{24,8},{28,20},{1,17},{... | collective-permute-start | bytes 884744 | tf_op jit(solution)/shard_map/ppermute | solution.py:224
  81.7 31.7 %collective-permute-start.31 = (bf16[96,1536]{1,0:T(8,128)(2,1)S(1)}, bf16[96,1536]{1,0:T(8,128)(2,1)S(1)}, u32[]{:S(2)}, u32[]{:S(2)}) collective-permute-start(bf16[96,1536]{1,0:T(8,128)(2,1)S(1)} %get-tuple-element.105.refs_1_), channel_id=1, source_target_pairs={{0,8},{4,20},{8,0},{12,28},{16,24},{20,4},{24,16},{28,12},{1,9},{5... | collective-permute-start | bytes 884744 | tf_op jit(solution)/shard_map/ppermute | solution.py:224
  97.8 17.5 %collective-permute-start.32 = (bf16[96,1536]{1,0:T(8,128)(2,1)S(1)}, bf16[96,1536]{1,0:T(8,128)(2,1)S(1)}, u32[]{:S(2)}, u32[]{:S(2)}) collective-permute-start(bf16[96,1536]{1,0:T(8,128)(2,1)S(1)} %get-tuple-element.105.refs_1_), channel_id=1, source_target_pairs={{0,4},{4,0},{8,12},{12,8},{16,20},{20,16},{24,28},{28,24},{1,5},{5... | collective-permute-start | bytes 884744 | tf_op jit(solution)/shard_map/ppermute | solution.py:224
  118.8 33.2 %collective-permute-start.8 = (bf16[192,1536]{1,0:T(8,128)(2,1)S(1)}, bf16[192,1536]{1,0:T(8,128)(2,1)S(1)}, u32[]{:S(2)}, u32[]{:S(2)}) collective-permute-start(bf16[192,1536]{1,0:T(8,128)(2,1)S(1)} %shard_map.75), channel_id=1, source_target_pairs={{0,16},{4,12},{8,24},{12,4},{16,0},{20,28},{24,8},{28,20},{1,17},{... | collective-permute-start | bytes 1769480 | tf_op jit(solution)/shard_map/ppermute | solution.py:224
  120.3 31.1 %collective-permute-start.38 = (bf16[144,1536]{1,0:T(8,128)(2,1)S(1)}, bf16[144,1536]{1,0:T(8,128)(2,1)S(1)}, u32[]{:S(2)}, u32[]{:S(2)}) collective-permute-start(bf16[144,1536]{1,0:T(8,128)(2,1)S(1)} %get-tuple-element.106.refs_1_), channel_id=1, source_target_pairs={{0,8},{4,20},{8,0},{12,28},{16,24},{20,4},{24,16},{28,12},{1,9},{5... | collective-permute-start | bytes 1327112 | tf_op jit(solution)/shard_map/ppermute | solution.py:224
  127.7 24.0 %collective-permute-start.36 = (bf16[144,1536]{1,0:T(8,128)(2,1)S(1)}, bf16[144,1536]{1,0:T(8,128)(2,1)S(1)}, u32[]{:S(2)}, u32[]{:S(2)}) collective-permute-start(bf16[144,1536]{1,0:T(8,128)(2,1)S(1)} %collective-permute-done.35.refs_2_), channel_id=1, source_target_pairs={{0,8},{4,20},{8,0},{12,28},{16,24},{20,4},{24,16},{28,12},{1,9},{5... | collective-permute-start | bytes 1327112 | tf_op jit(solution)/shard_map/ppermute | solution.py:224
  129.8 21.4 %collective-permute-start.56 = (bf16[96,1536]{1,0:T(8,128)(2,1)S(1)}, bf16[96,1536]{1,0:T(8,128)(2,1)S(1)}, u32[]{:S(2)}, u32[]{:S(2)}) collective-permute-start(bf16[96,1536]{1,0:T(8,128)(2,1)S(1)} %collective-permute-done.30.refs_2_), channel_id=1, source_target_pairs={{0,8},{4,20},{8,0},{12,28},{16,24},{20,4},{24,16},{28,12},{1,9},{5... | collective-permute-start | bytes 884744 | tf_op jit(solution)/shard_map/ppermute | solution.py:224
  130.7 21.5 %collective-permute-start.14 = (bf16[192,1536]{1,0:T(8,128)(2,1)S(1)}, bf16[192,1536]{1,0:T(8,128)(2,1)S(1)}, u32[]{:S(2)}, u32[]{:S(2)}) collective-permute-start(bf16[192,1536]{1,0:T(8,128)(2,1)S(1)} %shard_map.83), channel_id=1, source_target_pairs={{0,16},{4,12},{8,24},{12,4},{16,0},{20,28},{24,8},{28,20},{1,17},{... | collective-permute-start | bytes 1769480 | tf_op jit(solution)/shard_map/ppermute | solution.py:224
  158.3 26.0 %collective-permute-start.49 = (bf16[192,1536]{1,0:T(8,128)(2,1)S(1)}, bf16[192,1536]{1,0:T(8,128)(2,1)S(1)}, u32[]{:S(2)}, u32[]{:S(2)}) collective-permute-start(bf16[192,1536]{1,0:T(8,128)(2,1)S(1)} %get-tuple-element.108.refs_1_), channel_id=1, source_target_pairs={{0,16},{4,12},{8,24},{12,4},{16,0},{20,28},{24,8},{28,20},{1,17},{... | collective-permute-start | bytes 1769480 | tf_op jit(solution)/shard_map/ppermute | solution.py:224
  159.2 26.5 %collective-permute-start.46 = (bf16[192,1536]{1,0:T(8,128)(2,1)S(1)}, bf16[192,1536]{1,0:T(8,128)(2,1)S(1)}, u32[]{:S(2)}, u32[]{:S(2)}) collective-permute-start(bf16[192,1536]{1,0:T(8,128)(2,1)S(1)} %get-tuple-element.107.refs_1_), channel_id=1, source_target_pairs={{0,4},{4,0},{8,12},{12,8},{16,20},{20,16},{24,28},{28,24},{1,5},{5... | collective-permute-start | bytes 1769480 | tf_op jit(solution)/shard_map/ppermute | solution.py:224
  159.2 27.0 %collective-permute-start.50 = (bf16[192,1536]{1,0:T(8,128)(2,1)S(1)}, bf16[192,1536]{1,0:T(8,128)(2,1)S(1)}, u32[]{:S(2)}, u32[]{:S(2)}) collective-permute-start(bf16[192,1536]{1,0:T(8,128)(2,1)S(1)} %get-tuple-element.108.refs_1_), channel_id=1, source_target_pairs={{0,8},{4,20},{8,0},{12,28},{16,24},{20,4},{24,16},{28,12},{1,9},{5... | collective-permute-start | bytes 1769480 | tf_op jit(solution)/shard_map/ppermute | solution.py:224
  186.3 38.7 %collective-permute-start.52 = (bf16[192,1536]{1,0:T(8,128)(2,1)S(1)}, bf16[192,1536]{1,0:T(8,128)(2,1)S(1)}, u32[]{:S(2)}, u32[]{:S(2)}) collective-permute-start(bf16[192,1536]{1,0:T(8,128)(2,1)S(1)} %collective-permute-done.49.refs_2_), channel_id=1, source_target_pairs={{0,4},{4,0},{8,12},{12,8},{16,20},{20,16},{24,28},{28,24},{1,5},{5... | collective-permute-start | bytes 1769480 | tf_op jit(solution)/shard_map/ppermute | solution.py:224
  186.8 38.2 %collective-permute-start.53 = (bf16[192,1536]{1,0:T(8,128)(2,1)S(1)}, bf16[192,1536]{1,0:T(8,128)(2,1)S(1)}, u32[]{:S(2)}, u32[]{:S(2)}) collective-permute-start(bf16[192,1536]{1,0:T(8,128)(2,1)S(1)} %collective-permute-done.50.refs_3_), channel_id=1, source_target_pairs={{0,4},{4,0},{8,12},{12,8},{16,20},{20,16},{24,28},{28,24},{1,5},{5... | collective-permute-start | bytes 1769480 | tf_op jit(solution)/shard_map/ppermute | solution.py:224
  194.1 33.3 %collective-permute-start.55 = (bf16[192,1536]{1,0:T(8,128)(2,1)S(1)}, bf16[192,1536]{1,0:T(8,128)(2,1)S(1)}, u32[]{:S(2)}, u32[]{:S(2)}) collective-permute-start(bf16[192,1536]{1,0:T(8,128)(2,1)S(1)} %collective-permute-done.54.refs_1_), channel_id=1, source_target_pairs={{0,4},{4,0},{8,12},{12,8},{16,20},{20,16},{24,28},{28,24},{1,5},{5... | collective-permute-start | bytes 1769480 | tf_op jit(solution)/shard_map/ppermute | solution.py:224
  200.4 29.9 %collective-permute-start.59 = (bf16[192,1536]{1,0:T(8,128)(2,1)S(1)}, bf16[192,1536]{1,0:T(8,128)(2,1)S(1)}, u32[]{:S(2)}, u32[]{:S(2)}) collective-permute-start(bf16[192,1536]{1,0:T(8,128)(2,1)S(1)} %collective-permute-done.58.refs_1_), channel_id=1, source_target_pairs={{0,4},{4,0},{8,12},{12,8},{16,20},{20,16},{24,28},{28,24},{1,5},{5... | collective-permute-start | bytes 1769480 | tf_op jit(solution)/shard_map/ppermute | solution.py:224
  200.4 28.5 %collective-permute-start.57 = (bf16[96,1536]{1,0:T(8,128)(2,1)S(1)}, bf16[96,1536]{1,0:T(8,128)(2,1)S(1)}, u32[]{:S(2)}, u32[]{:S(2)}) collective-permute-start(bf16[96,1536]{1,0:T(8,128)(2,1)S(1)} %collective-permute-done.56.refs_1_), channel_id=1, source_target_pairs={{0,4},{4,0},{8,12},{12,8},{16,20},{20,16},{24,28},{28,24},{1,5},{5... | collective-permute-start | bytes 884744 | tf_op jit(solution)/shard_map/ppermute | solution.py:224
  (36 other events, 319.0 us)

commit v3 on v2

--- a/solution.py
+++ b/solution.py
@@ -16,18 +16,30 @@
 softness = 0.05
 
 UNITS = 16
-CHUNKS = (2, 3, 4, 4, 2, 1)
+CHUNKS = (2, 3, 4, 3, 3, 1)
+LOADS = (
+    ("ca0",),
+    ("oa0", "ca1"),
+    ("cb0", "oa1", "cb5", "oa5"),
+    ("ob0", "ob1", "ca3", "oa3", "ca4", "oa4", "ca5"),
+    ("mm0", "cb1", "ob5"),
+    ("ca2", "oa2", "cb3", "ob3"),
+    ("mm1", "cb2", "ob2", "mm3", "cb4", "ob4", "mm5"),
+    ("mm2", "mm4"),
+)
 ORDER = (
-    "ld0", "d0", "ld1", "d1", "comb0", "R0", "ld2", "comb1", "d2", "R1", "sec0", "r0", "ld3", "comb2", "R2",
-    "sec1", "r1", "ld4", "d4", "upd0", "b0", "d3", "ld6", "a0", "upd1", "ld5", "comb4", "R4", "d5", "comb5",
-    "R5", "comb3", "R3", "st0", "o0", "f0", "sec4", "r4", "upd4", "sec5", "r5", "ld7", "upd5", "a5", "A0",
-    "b5", "a1", "st5", "sec2", "A5", "r2", "o4", "sec3", "r3", "f5", "B0", "upd2", "a2", "o5", "F5", "pf5",
-    "a4", "upd3", "o3", "a3", "pa0", "st3", "A1", "b4", "b1", "f1", "st4", "o1", "A2", "b3", "st2", "A4",
-    "B4", "f4", "B5", "pa5", "b2", "f2", "pa4", "A3", "F1", "pf1", "B3", "o2", "f3", "F0", "B1", "pa1", "F4",
-    "pf0", "B2", "pa3", "pa2", "F2", "st1", "pf2", "F3", "pf4", "pf3",
+    "ld0", "da0", "ld1", "comb0", "R0", "da1", "ld2", "comb1", "R1", "ld3", "da5", "da3", "da4", "comb5",
+    "db0", "sec0", "r0", "comb4", "R5", "comb3", "R3", "ld4", "upd0", "st0", "o0", "R4", "db5", "a0", "db1",
+    "sec1", "r1", "sec5", "r5", "ld5", "da2", "comb2", "R2", "db3", "sec3", "r3", "ld6", "upd1", "st1",
+    "upd5", "b5", "upd3", "st5", "st3", "a5", "db4", "sec4", "r4", "db2", "sec2", "r2", "a1", "a3", "ld7",
+    "upd2", "st2", "upd4", "b3", "o5", "o3", "A0", "f5", "st4", "a4", "b0", "b1", "B3", "A3", "pa3", "F5",
+    "pf5", "f3", "f0", "A5", "a2", "B5", "B0", "pa0", "pa5", "o1", "A1", "B1", "b4", "pa1", "A4", "f1", "F3",
+    "pf3", "o4", "f2", "b2", "B4", "pa4", "o2", "F1", "F0", "pf1", "A2", "f4", "F2", "pf0", "pf2", "B2",
+    "pa2", "F4", "pf4",
 )
 MOVES = {
-    "d": ("cut", "across"),
+    "da": ("ca", "across"),
+    "db": ("cb", "across"),
     "R": ("comb", "first"),
     "r": ("sec", "second"),
     "a": ("upd", "second"),
@@ -38,6 +50,12 @@
     "B": ("b", "across"),
     "F": ("f", "across"),
 }
+TILES = {
+    "oa": ((1, 0), (3, 0)),
+    "ob": ((0, 0), (2, 0)),
+    "ca": ((2, 1), (3, 1)),
+    "cb": ((0, 1), (1, 1)),
+}
 SOURCES = {"pa": ("upd", "a", "b", "o", "A", "B"), "pf": ("f", "F")}
 PLACED = {"pa": ((0, 0), (2, 0), (1, 0), (0, 1), (1, 1), (2, 1)), "pf": ((3, 0), (3, 1))}
 ROWS = 16
@@ -91,30 +109,22 @@
             for src in (master_ref, momentum_ref):
                 pairs.append((at(src, row0, rows), outs.pop(0)))
         else:
-            core = s_ref[0] % 2
-            held = core if kind == "own" else 1 - core
             dst = outs.pop(0)
-            for m in range(4):
-                pairs.append((at(grad_ref, (2 * m + held) * tile + row0, rows), at(dst, m * rows, rows)))
+            for i, t in enumerate(TILES[kind]):
+                pairs.append((at(grad_ref, (s_ref[t[0]] ^ t[1]) * tile + row0, rows), at(dst, i * rows, rows)))
     run_copies(pairs, sem)
 
 
 def combine_kernel(rows, s_ref, own_ref, peer_ref, out_ref):
-    for j in range(2):
-        base = (s_ref[1 + 2 * j] // 2) * rows
-
-        def body(row):
-            total = f32(own_ref, base + row) + f32(peer_ref, base + row)
-            out_ref[pl.ds(j * rows + row, ROWS), :] = total.astype(jnp.bfloat16)
-
-        rows_loop(rows, body)
+    def body(row):
+        out_ref[pl.ds(row, ROWS), :] = (f32(own_ref, row) + f32(peer_ref, row)).astype(jnp.bfloat16)
+
+    rows_loop(2 * rows, body)
 
 
 def second_kernel(rows, s_ref, own_ref, peer_ref, recv_ref, out_ref):
-    base = (s_ref[2] // 2) * rows
-
     def body(row):
-        total = f32(own_ref, base + row) + f32(peer_ref, base + row) + f32(recv_ref, rows + row)
+        total = f32(own_ref, rows + row) + f32(peer_ref, rows + row) + f32(recv_ref, rows + row)
         out_ref[pl.ds(row, ROWS), :] = total.astype(jnp.bfloat16)
 
     rows_loop(rows, body)
@@ -122,10 +132,9 @@
 
 def update_kernel(rows, scale, s_ref, own_ref, peer_ref, first_ref, second_ref, master_ref, momentum_ref, *outs):
     new_master_ref, new_momentum_ref, weights_ref = outs
-    base = (s_ref[0] // 2) * rows
 
     def body(row):
-        summed = (f32(own_ref, base + row) + f32(peer_ref, base + row)) + (f32(first_ref, row) + f32(second_ref, row))
+        summed = (f32(own_ref, row) + f32(peer_ref, row)) + (f32(first_ref, row) + f32(second_ref, row))
         here = pl.ds(row, ROWS)
         new_master, new_momentum = lion_update(summed * scale, master_ref[here, :], momentum_ref[here, :])
         new_master_ref[here, :] = new_master
@@ -195,12 +204,15 @@
             compiler_params=pltpu.CompilerParams(vmem_limit_bytes=VMEM_LIMIT),
         )(tiles, *args)
 
+    def split(name):
+        return name.rstrip(string.digits), int(name.lstrip(string.ascii_letters))
+
     def load(names):
         jobs, outs, copies = [], [], 0
         for kind, k in names:
             jobs.append((kind, sizes[k], starts[k]))
-            outs += [near(sizes[k], jnp.float32)] * 2 if kind == "mm" else [near(4 * sizes[k])]
-            copies += 2 if kind == "mm" else 4
+            outs += [near(sizes[k], jnp.float32)] * 2 if kind == "mm" else [near(2 * sizes[k])]
+            copies += 2
         kernel = functools.partial(load_kernel, jobs, tile)
         got = list(call(kernel, scal, [grad, master, momentum], [], outs, copies))
         for kind, k in names:
@@ -214,26 +226,26 @@
 
     weights_shape = [pltpu.HBM((total_rows, cols), bf)]
     state_shape = [pltpu.HBM((tile, cols), jnp.float32)] * 2
-    held, weights, state, last = {}, [], [], len(CHUNKS)
+    held, weights, state = {}, [], []
     for name in ORDER:
-        kind, k = name.rstrip(string.digits), int(name.lstrip(string.ascii_letters))
-        rows = sizes[k] if k < last else 0
+        kind, k = split(name)
+        rows = sizes[k] if kind != "ld" else 0
         get = lambda *kinds: [held[kind, k] for kind in kinds]
         if kind in MOVES:
             source, how = MOVES[kind]
             held[kind, k] = lax.ppermute(held[source, k], "dp", perms[how])
         elif kind == "ld":
-            load([(what, k - i) for i, what in enumerate(("cut", "own", "mm")) if 0 <= k - i < last])
+            load([split(what) for what in LOADS[k]])
         elif kind == "comb":
             kernel = functools.partial(combine_kernel, rows)
-            (held[kind, k],) = call(kernel, scal, [], get("own", "d"), [near(2 * rows)])
+            (held[kind, k],) = call(kernel, scal, [], get("oa", "da"), [near(2 * rows)])
         elif kind == "sec":
             kernel = functools.partial(second_kernel, rows)
-            (held[kind, k],) = call(kernel, scal, [], get("own", "d", "R"), [near(rows)])
+            (held[kind, k],) = call(kernel, scal, [], get("ob", "db", "R"), [near(rows)])
         elif kind == "upd":
             kernel = functools.partial(update_kernel, rows, 1.0 / replicas)
             outs = [near(rows, jnp.float32), near(rows, jnp.float32), near(rows)]
-            args = get("own", "d", "R", "r") + held["mm", k]
+            args = get("ob", "db", "R", "r") + held["mm", k]
             *held["new", k], held[kind, k] = call(kernel, scal, [], args, outs, 0, {5: 0, 6: 1})
         elif kind == "st":
             kernel = functools.partial(store_kernel, rows, starts[k])

time: 232 us -> 227 us (0.978)
  waiting for transfers between devices: 123 us -> 111 us
  starting transfers between devices: 38.8 us -> 46.2 us
    ppermute x60 -> x66, waiting for transfers between devices: 123 us -> 111 us  [per_device(): held[kind, k] = lax.ppermute(held[source, k], 'dp', perms[how])]
    ppermute x60 -> x66, starting transfers between devices: 38.8 us -> 46.2 us  [per_device(): held[kind, k] = lax.ppermute(held[source, k], 'dp', perms[how])]
  transfers between devices with their start and end apart: 60 -> 66, of which waited for: 18 -> 18; matrix products, arithmetic and copies ran while one was open for 0% -> 0% of each run, Pallas kernels for 27% -> 28%
where the time goes in v3:
time: 227 us
  waiting for transfers between devices  111 us (49%)
  Pallas kernels  68.2 us (30%)
  starting transfers between devices  46.2 us (20%)
    ppermute x66, waiting for transfers between devices, per_device(): held[kind, k] = lax.ppermute(held[source, k], 'dp', perms[how])  111 us
    pallas_call x44, Pallas kernels, call(): pl.pallas_call(kernel, grid_spec=pltpu.PrefetchScalarGridSpec(num_scalar_...  68.2 us
    ppermute x66, starting transfers between devices, per_device(): held[kind, k] = lax.ppermute(held[source, k], 'dp', perms[how])  46.2 us
  transfers between devices with their start and end apart: 66, of which 18 were waited for; matrix products, arithmetic and copies ran while one was open for 0% of the time, Pallas kernels for 28%

profile of v3, /device:TPU:0, one launch (start us, length us, event | category | flops | bytes accessed | tf_op | source)
XLA Modules:
  0.0 226.7 jit_solution(387029732769834124)
XLA Ops:
  0.7 2.2 shard_map.64
  3.5 3.2 %shard_map.58 = (bf16[192,1536]{1,0:T(8,128)(2,1)S(1)}, bf16[288,1536]{1,0:T(8,128)(2,1)S(1)}, bf16[288,1536]{1,0:T(8,128)(2,1)S(1)}, bf16[288,1536]{1,0:T(8,128...) custom-call(s32[4]{0:T(128)S(1)} %pad_add_fusion.s_ref, ...), custom_call_target="tpu_custom_call" | custom-call | tf_op jit(solution)/shard_map/pallas_call | solution.py:193
  12.2 2.6 %collective-permute-start.10 = (bf16[96,1536]{1,0:T(8,128)(2,1)S(1)}, bf16[96,1536]{1,0:T(8,128)(2,1)S(1)}, u32[]{:S(2)}, u32[]{:S(2)}) collective-permute-start(bf16[96,1536]{1,0:T(8,128)(2,1)S(1)} %shard_map.72), channel_id=1, source_target_pairs={{0,8},{4,20},{8,0},{12,28},{16,24},{20,4},{24,16},{28,12},{1,9},{5... | collective-permute-start | bytes 884744 | tf_op jit(solution)/shard_map/ppermute | solution.py:236
  17.0 2.5 %collective-permute-done.10.recv_ref.first_ref = bf16[96,1536]{1,0:T(8,128)(2,1)S(1)} collective-permute-done((bf16[96,1536]{1,0:T(8,128)(2,1)S(1)}, bf16[96,1536]{1,0:T(8,128)(2,1)S(1)}, u32[]{:S(2)}, u32[]{:S(2)}) %collective-permute-start.10) | collective-permute-done | bytes 294944 | tf_op jit(solution)/shard_map/ppermute | solution.py:236
  20.1 2.1 collective-permute-start.11
  22.2 2.7 %shard_map.76 = (bf16[384,1536]{1,0:T(8,128)(2,1)S(1)}, bf16[384,1536]{1,0:T(8,128)(2,1)S(1)}, bf16[288,1536]{1,0:T(8,128)(2,1)S(1)}, bf16[288,1536]{1,0:T(8,128)(2,1)S(1)}) custom-call(s32[4]{0:T(128)S(1)} %pad_add_fusion.s_ref, bf16[6144,1536]{1,0:T(8,128)(2,1)} %bitcast.16, f32[768,1536]{1,0:T(8,128)} %bitcast.24, f32[768,1536]{1,0:T(8,128)} %bitcast.32), custom_call_target="tpu_custom_call" | custom-call | tf_op jit(solution)/shard_map/pallas_call | solution.py:193
  25.6 4.1 %shard_map.69 = (f32[144,1536]{1,0:T(8,128)S(1)}, f32[144,1536]{1,0:T(8,128)S(1)}, bf16[384,1536]{1,0:T(8,128)(2,1)S(1)}, bf16[384,1536]{1,0:T(8,128)(2,1)S(1)},...) custom-call(s32[4]{0:T(128)S(1)} %pad_add_fusion.s_ref, ...), custom_call_target="tpu_custom_call" | custom-call | tf_op jit(solution)/shard_map/pallas_call | solution.py:193
  35.7 4.4 %collective-permute-done.29.refs_2_ = bf16[48,1536]{1,0:T(8,128)(2,1)S(1)} collective-permute-done((bf16[48,1536]{1,0:T(8,128)(2,1)S(1)}, bf16[48,1536]{1,0:T(8,128)(2,1)S(1)}, u32[]{:S(2)}, u32[]{:S(2)}) %collective-permute-start.29) | collective-permute-done | bytes 147488 | tf_op jit(solution)/shard_map/ppermute | solution.py:236
  40.2 4.0 %collective-permute-done.37.refs_3_ = bf16[48,1536]{1,0:T(8,128)(2,1)S(1)} collective-permute-done((bf16[48,1536]{1,0:T(8,128)(2,1)S(1)}, bf16[48,1536]{1,0:T(8,128)(2,1)S(1)}, u32[]{:S(2)}, u32[]{:S(2)}) %collective-permute-start.37) | collective-permute-done | bytes 147488 | tf_op jit(solution)/shard_map/ppermute | solution.py:236
  46.8 2.5 %collective-permute-done.30.refs_1_ = bf16[48,1536]{1,0:T(8,128)(2,1)S(1)} collective-permute-done((bf16[48,1536]{1,0:T(8,128)(2,1)S(1)}, bf16[48,1536]{1,0:T(8,128)(2,1)S(1)}, u32[]{:S(2)}, u32[]{:S(2)}) %collective-permute-start.30) | collective-permute-done | bytes 147488 | tf_op jit(solution)/shard_map/ppermute | solution.py:236
  54.3 4.1 %collective-permute-done.3.second_ref = bf16[96,1536]{1,0:T(8,128)(2,1)S(1)} collective-permute-done((bf16[96,1536]{1,0:T(8,128)(2,1)S(1)}, bf16[96,1536]{1,0:T(8,128)(2,1)S(1)}, u32[]{:S(2)}, u32[]{:S(2)}) %collective-permute-start.3) | collective-permute-done | bytes 294944 | tf_op jit(solution)/shard_map/ppermute | solution.py:236
  62.7 4.0 %collective-permute-done.6.recv_ref.first_ref = bf16[288,1536]{1,0:T(8,128)(2,1)S(1)} collective-permute-done((bf16[288,1536]{1,0:T(8,128)(2,1)S(1)}, bf16[288,1536]{1,0:T(8,128)(2,1)S(1)}, u32[]{:S(2)}, u32[]{:S(2)}) %collective-permute-start.6) | collective-permute-done | bytes 884768 | tf_op jit(solution)/shard_map/ppermute | solution.py:236
  68.3 7.8 %collective-permute-done.14.recv_ref.first_ref = bf16[288,1536]{1,0:T(8,128)(2,1)S(1)} collective-permute-done((bf16[288,1536]{1,0:T(8,128)(2,1)S(1)}, bf16[288,1536]{1,0:T(8,128)(2,1)S(1)}, u32[]{:S(2)}, u32[]{:S(2)}) %collective-permute-start.14) | collective-permute-done | bytes 884768 | tf_op jit(solution)/shard_map/ppermute | solution.py:236
  78.2 7.4 %collective-permute-done.22.recv_ref.first_ref = bf16[288,1536]{1,0:T(8,128)(2,1)S(1)} collective-permute-done((bf16[288,1536]{1,0:T(8,128)(2,1)S(1)}, bf16[288,1536]{1,0:T(8,128)(2,1)S(1)}, u32[]{:S(2)}, u32[]{:S(2)}) %collective-permute-start.22) | collective-permute-done | bytes 884768 | tf_op jit(solution)/shard_map/ppermute | solution.py:236
  88.0 13.4 %collective-permute-done.33.refs_3_ = bf16[96,1536]{1,0:T(8,128)(2,1)S(1)} collective-permute-done((bf16[96,1536]{1,0:T(8,128)(2,1)S(1)}, bf16[96,1536]{1,0:T(8,128)(2,1)S(1)}, u32[]{:S(2)}, u32[]{:S(2)}) %collective-permute-start.33) | collective-permute-done | bytes 294944 | tf_op jit(solution)/shard_map/ppermute | solution.py:236
  108.2 3.1 %collective-permute-done.15.second_ref = bf16[144,1536]{1,0:T(8,128)(2,1)S(1)} collective-permute-done((bf16[144,1536]{1,0:T(8,128)(2,1)S(1)}, bf16[144,1536]{1,0:T(8,128)(2,1)S(1)}, u32[]{:S(2)}, u32[]{:S(2)}) %collective-permute-start.15) | collective-permute-done | bytes 442400 | tf_op jit(solution)/shard_map/ppermute | solution.py:236
  113.0 3.0 %collective-permute-done.7.second_ref = bf16[144,1536]{1,0:T(8,128)(2,1)S(1)} collective-permute-done((bf16[144,1536]{1,0:T(8,128)(2,1)S(1)}, bf16[144,1536]{1,0:T(8,128)(2,1)S(1)}, u32[]{:S(2)}, u32[]{:S(2)}) %collective-permute-start.7) | collective-permute-done | bytes 442400 | tf_op jit(solution)/shard_map/ppermute | solution.py:236
  117.5 5.8 %collective-permute-done.23.second_ref = bf16[144,1536]{1,0:T(8,128)(2,1)S(1)} collective-permute-done((bf16[144,1536]{1,0:T(8,128)(2,1)S(1)}, bf16[144,1536]{1,0:T(8,128)(2,1)S(1)}, u32[]{:S(2)}, u32[]{:S(2)}) %collective-permute-start.23) | collective-permute-done | bytes 442400 | tf_op jit(solution)/shard_map/ppermute | solution.py:236
  127.4 4.1 %collective-permute-done.24.refs_1_ = bf16[144,1536]{1,0:T(8,128)(2,1)S(1)} collective-permute-done((bf16[144,1536]{1,0:T(8,128)(2,1)S(1)}, bf16[144,1536]{1,0:T(8,128)(2,1)S(1)}, u32[]{:S(2)}, u32[]{:S(2)}) %collective-permute-start.24) | collective-permute-done | bytes 442400 | tf_op jit(solution)/shard_map/ppermute | solution.py:236
  131.8 2.7 %shard_map.83 = (f32[192,1536]{1,0:T(8,128)S(1)}, f32[192,1536]{1,0:T(8,128)S(1)}, f32[144,1536]{1,0:T(8,128)S(1)}, f32[144,1536]{1,0:T(8,128)S(1)}) custom-call(s32[4]{0:T(128)S(1)} %pad_add_fusion.s_ref, bf16[6144,1536]{1,0:T(8,128)(2,1)} %bitcast.18, f32[768,1536]{1,0:T(8,128)} %bitcast.26, f32[768,1536]{1,0:T(8,128)} %bitcast.34), custom_call_target="tpu_custom_call" | custom-call | tf_op jit(solution)/shard_map/pallas_call | solution.py:193
  141.7 13.8 %collective-permute-done.48.refs_2_ = bf16[144,1536]{1,0:T(8,128)(2,1)S(1)} collective-permute-done((bf16[144,1536]{1,0:T(8,128)(2,1)S(1)}, bf16[144,1536]{1,0:T(8,128)(2,1)S(1)}, u32[]{:S(2)}, u32[]{:S(2)}) %collective-permute-start.48) | collective-permute-done | bytes 442400 | tf_op jit(solution)/shard_map/ppermute | solution.py:236
  161.6 12.1 %collective-permute-done.57.refs_2_ = bf16[192,1536]{1,0:T(8,128)(2,1)S(1)} collective-permute-done((bf16[192,1536]{1,0:T(8,128)(2,1)S(1)}, bf16[192,1536]{1,0:T(8,128)(2,1)S(1)}, u32[]{:S(2)}, u32[]{:S(2)}) %collective-permute-start.57) | collective-permute-done | bytes 589856 | tf_op jit(solution)/shard_map/ppermute | solution.py:236
  178.0 16.6 %collective-permute-done.64.refs_1_ = bf16[144,1536]{1,0:T(8,128)(2,1)S(1)} collective-permute-done((bf16[144,1536]{1,0:T(8,128)(2,1)S(1)}, bf16[144,1536]{1,0:T(8,128)(2,1)S(1)}, u32[]{:S(2)}, u32[]{:S(2)}) %collective-permute-start.64) | collective-permute-done | bytes 442400 | tf_op jit(solution)/shard_map/ppermute | solution.py:236
  222.9 2.4 %shard_map.100.refs_0_ = bf16[6144,1536]{1,0:T(8,128)(2,1)} custom-call(s32[4]{0:T(128)S(1)} %pad_add_fusion.s_ref, bf16[6144,1536]{1,0:T(8,128)(2,1)} %shard_map.99.refs_0_, bf16[192,1536]{1,0:T(8,128)(2,1)S(1)} %get-tuple-element.132.refs_1_, bf16[192,1536]{1,0:T(8,128)(2,1)S(1)} %collective-permute-done.57.refs_2_, ...), custom_call_target="tpu_custom_call", output_to_operand_aliasing={{}: (1, {})} | custom-call | tf_op jit(solution)/shard_map/pallas_call | solution.py:193
  (153 shorter events, 94.9 us)
Async XLA Ops:
  2.9 26.9 %collective-permute-start.4 = (bf16[288,1536]{1,0:T(8,128)(2,1)S(1)}, bf16[288,1536]{1,0:T(8,128)(2,1)S(1)}, u32[]{:S(2)}, u32[]{:S(2)}) collective-permute-start(bf16[288,1536]{1,0:T(8,128)(2,1)S(1)} %get-tuple-element.78), channel_id=1, source_target_pairs={{0,4},{4,0},{8,12},{12,8},{16,20},{20,16},{24,28},{28,24},{1,5},{5... | collective-permute-start | bytes 2654216 | tf_op jit(solution)/shard_map/ppermute | solution.py:236
  33.9 26.9 %collective-permute-start.17 = (bf16[384,1536]{1,0:T(8,128)(2,1)S(1)}, bf16[384,1536]{1,0:T(8,128)(2,1)S(1)}, u32[]{:S(2)}, u32[]{:S(2)}) collective-permute-start(bf16[384,1536]{1,0:T(8,128)(2,1)S(1)} %get-tuple-element.110), channel_id=1, source_target_pairs={{0,4},{4,0},{8,12},{12,8},{16,20},{20,16},{24,28},{28,24},{1,5},{5... | collective-permute-start | bytes 3538952 | tf_op jit(solution)/shard_map/ppermute | solution.py:236
  40.2 21.7 %collective-permute-start.16 = (bf16[384,1536]{1,0:T(8,128)(2,1)S(1)}, bf16[384,1536]{1,0:T(8,128)(2,1)S(1)}, u32[]{:S(2)}, u32[]{:S(2)}) collective-permute-start(bf16[384,1536]{1,0:T(8,128)(2,1)S(1)} %get-tuple-element.108), channel_id=1, source_target_pairs={{0,4},{4,0},{8,12},{12,8},{16,20},{20,16},{24,28},{28,24},{1,5},{5... | collective-permute-start | bytes 3538952 | tf_op jit(solution)/shard_map/ppermute | solution.py:236
  53.0 23.2 %collective-permute-start.14 = (bf16[288,1536]{1,0:T(8,128)(2,1)S(1)}, bf16[288,1536]{1,0:T(8,128)(2,1)S(1)}, u32[]{:S(2)}, u32[]{:S(2)}) collective-permute-start(bf16[288,1536]{1,0:T(8,128)(2,1)S(1)} %shard_map.77), channel_id=1, source_target_pairs={{0,8},{4,20},{8,0},{12,28},{16,24},{20,4},{24,16},{28,12},{1,9},{5... | collective-permute-start | bytes 2654216 | tf_op jit(solution)/shard_map/ppermute | solution.py:236
  58.4 27.2 %collective-permute-start.22 = (bf16[288,1536]{1,0:T(8,128)(2,1)S(1)}, bf16[288,1536]{1,0:T(8,128)(2,1)S(1)}, u32[]{:S(2)}, u32[]{:S(2)}) collective-permute-start(bf16[288,1536]{1,0:T(8,128)(2,1)S(1)} %shard_map.86), channel_id=1, source_target_pairs={{0,8},{4,20},{8,0},{12,28},{16,24},{20,4},{24,16},{28,12},{1,9},{5... | collective-permute-start | bytes 2654216 | tf_op jit(solution)/shard_map/ppermute | solution.py:236
  61.9 63.1 %collective-permute-start.18 = (bf16[384,1536]{1,0:T(8,128)(2,1)S(1)}, bf16[384,1536]{1,0:T(8,128)(2,1)S(1)}, u32[]{:S(2)}, u32[]{:S(2)}) collective-permute-start(bf16[384,1536]{1,0:T(8,128)(2,1)S(1)} %shard_map.81), channel_id=1, source_target_pairs={{0,8},{4,20},{8,0},{12,28},{16,24},{20,4},{24,16},{28,12},{1,9},{5... | collective-permute-start | bytes 3538952 | tf_op jit(solution)/shard_map/ppermute | solution.py:236
  66.7 34.8 %collective-permute-start.33 = (bf16[96,1536]{1,0:T(8,128)(2,1)S(1)}, bf16[96,1536]{1,0:T(8,128)(2,1)S(1)}, u32[]{:S(2)}, u32[]{:S(2)}) collective-permute-start(bf16[96,1536]{1,0:T(8,128)(2,1)S(1)} %get-tuple-element.129.refs_1_), channel_id=1, source_target_pairs={{0,8},{4,20},{8,0},{12,28},{16,24},{20,4},{24,16},{28,12},{1,9},{5... | collective-permute-start | bytes 884744 | tf_op jit(solution)/shard_map/ppermute | solution.py:236
  76.2 27.8 %collective-permute-start.34 = (bf16[96,1536]{1,0:T(8,128)(2,1)S(1)}, bf16[96,1536]{1,0:T(8,128)(2,1)S(1)}, u32[]{:S(2)}, u32[]{:S(2)}) collective-permute-start(bf16[96,1536]{1,0:T(8,128)(2,1)S(1)} %get-tuple-element.129.refs_1_), channel_id=1, source_target_pairs={{0,4},{4,0},{8,12},{12,8},{16,20},{20,16},{24,28},{28,24},{1,5},{5... | collective-permute-start | bytes 884744 | tf_op jit(solution)/shard_map/ppermute | solution.py:236
  78.2 26.8 %collective-permute-start.35 = (bf16[96,1536]{1,0:T(8,128)(2,1)S(1)}, bf16[96,1536]{1,0:T(8,128)(2,1)S(1)}, u32[]{:S(2)}, u32[]{:S(2)}) collective-permute-start(bf16[96,1536]{1,0:T(8,128)(2,1)S(1)} %collective-permute-done.32.refs_2_), channel_id=1, source_target_pairs={{0,4},{4,0},{8,12},{12,8},{16,20},{20,16},{24,28},{28,24},{1,5},{5... | collective-permute-start | bytes 884744 | tf_op jit(solution)/shard_map/ppermute | solution.py:236
  85.6 21.3 %collective-permute-start.55 = (bf16[96,1536]{1,0:T(8,128)(2,1)S(1)}, bf16[96,1536]{1,0:T(8,128)(2,1)S(1)}, u32[]{:S(2)}, u32[]{:S(2)}) collective-permute-start(bf16[96,1536]{1,0:T(8,128)(2,1)S(1)} %collective-permute-done.32.refs_2_), channel_id=1, source_target_pairs={{0,8},{4,20},{8,0},{12,28},{16,24},{20,4},{24,16},{28,12},{1,9},{5... | collective-permute-start | bytes 884744 | tf_op jit(solution)/shard_map/ppermute | solution.py:236
  105.1 18.2 %collective-permute-start.23 = (bf16[144,1536]{1,0:T(8,128)(2,1)S(1)}, bf16[144,1536]{1,0:T(8,128)(2,1)S(1)}, u32[]{:S(2)}, u32[]{:S(2)}) collective-permute-start(bf16[144,1536]{1,0:T(8,128)(2,1)S(1)} %shard_map.87), channel_id=1, source_target_pairs={{0,16},{4,12},{8,24},{12,4},{16,0},{20,28},{24,8},{28,20},{1,17},{... | collective-permute-start | bytes 1327112 | tf_op jit(solution)/shard_map/ppermute | solution.py:236
  112.7 18.8 %collective-permute-start.24 = (bf16[144,1536]{1,0:T(8,128)(2,1)S(1)}, bf16[144,1536]{1,0:T(8,128)(2,1)S(1)}, u32[]{:S(2)}, u32[]{:S(2)}) collective-permute-start(bf16[144,1536]{1,0:T(8,128)(2,1)S(1)} %get-tuple-element.127.refs_0_), channel_id=1, source_target_pairs={{0,16},{4,12},{8,24},{12,4},{16,0},{20,28},{24,8},{28,20},{1,17},{... | collective-permute-start | bytes 1327112 | tf_op jit(solution)/shard_map/ppermute | solution.py:236
  131.5 24.0 %collective-permute-start.19 = (bf16[192,1536]{1,0:T(8,128)(2,1)S(1)}, bf16[192,1536]{1,0:T(8,128)(2,1)S(1)}, u32[]{:S(2)}, u32[]{:S(2)}) collective-permute-start(bf16[192,1536]{1,0:T(8,128)(2,1)S(1)} %shard_map.82), channel_id=1, source_target_pairs={{0,16},{4,12},{8,24},{12,4},{16,0},{20,28},{24,8},{28,20},{1,17},{... | collective-permute-start | bytes 1769480 | tf_op jit(solution)/shard_map/ppermute | solution.py:236
  135.9 19.6 %collective-permute-start.48 = (bf16[144,1536]{1,0:T(8,128)(2,1)S(1)}, bf16[144,1536]{1,0:T(8,128)(2,1)S(1)}, u32[]{:S(2)}, u32[]{:S(2)}) collective-permute-start(bf16[144,1536]{1,0:T(8,128)(2,1)S(1)} %get-tuple-element.131.refs_1_), channel_id=1, source_target_pairs={{0,16},{4,12},{8,24},{12,4},{16,0},{20,28},{24,8},{28,20},{1,17},{... | collective-permute-start | bytes 1327112 | tf_op jit(solution)/shard_map/ppermute | solution.py:236
  139.7 18.0 %collective-permute-start.49 = (bf16[144,1536]{1,0:T(8,128)(2,1)S(1)}, bf16[144,1536]{1,0:T(8,128)(2,1)S(1)}, u32[]{:S(2)}, u32[]{:S(2)}) collective-permute-start(bf16[144,1536]{1,0:T(8,128)(2,1)S(1)} %get-tuple-element.131.refs_1_), channel_id=1, source_target_pairs={{0,8},{4,20},{8,0},{12,28},{16,24},{20,4},{24,16},{28,12},{1,9},{5... | collective-permute-start | bytes 1327112 | tf_op jit(solution)/shard_map/ppermute | solution.py:236
  173.7 20.9 %collective-permute-start.58 = (bf16[192,1536]{1,0:T(8,128)(2,1)S(1)}, bf16[192,1536]{1,0:T(8,128)(2,1)S(1)}, u32[]{:S(2)}, u32[]{:S(2)}) collective-permute-start(bf16[192,1536]{1,0:T(8,128)(2,1)S(1)} %collective-permute-done.57.refs_2_), channel_id=1, source_target_pairs={{0,8},{4,20},{8,0},{12,28},{16,24},{20,4},{24,16},{28,12},{1,9},{5... | collective-permute-start | bytes 1769480 | tf_op jit(solution)/shard_map/ppermute | solution.py:236
  175.4 19.8 %collective-permute-start.60 = (bf16[192,1536]{1,0:T(8,128)(2,1)S(1)}, bf16[192,1536]{1,0:T(8,128)(2,1)S(1)}, u32[]{:S(2)}, u32[]{:S(2)}) collective-permute-start(bf16[192,1536]{1,0:T(8,128)(2,1)S(1)} %get-tuple-element.132.refs_1_), channel_id=1, source_target_pairs={{0,8},{4,20},{8,0},{12,28},{16,24},{20,4},{24,16},{28,12},{1,9},{5... | collective-permute-start | bytes 1769480 | tf_op jit(solution)/shard_map/ppermute | solution.py:236
  175.7 18.9 %collective-permute-start.64 = (bf16[144,1536]{1,0:T(8,128)(2,1)S(1)}, bf16[144,1536]{1,0:T(8,128)(2,1)S(1)}, u32[]{:S(2)}, u32[]{:S(2)}) collective-permute-start(bf16[144,1536]{1,0:T(8,128)(2,1)S(1)} %collective-permute-done.48.refs_2_), channel_id=1, source_target_pairs={{0,8},{4,20},{8,0},{12,28},{16,24},{20,4},{24,16},{28,12},{1,9},{5... | collective-permute-start | bytes 1327112 | tf_op jit(solution)/shard_map/ppermute | solution.py:236
  177.5 18.2 %collective-permute-start.54 = (bf16[144,1536]{1,0:T(8,128)(2,1)S(1)}, bf16[144,1536]{1,0:T(8,128)(2,1)S(1)}, u32[]{:S(2)}, u32[]{:S(2)}) collective-permute-start(bf16[144,1536]{1,0:T(8,128)(2,1)S(1)} %collective-permute-done.53.refs_1_), channel_id=1, source_target_pairs={{0,4},{4,0},{8,12},{12,8},{16,20},{20,16},{24,28},{28,24},{1,5},{5... | collective-permute-start | bytes 1327112 | tf_op jit(solution)/shard_map/ppermute | solution.py:236
  194.6 28.2 %collective-permute-start.61 = (bf16[192,1536]{1,0:T(8,128)(2,1)S(1)}, bf16[192,1536]{1,0:T(8,128)(2,1)S(1)}, u32[]{:S(2)}, u32[]{:S(2)}) collective-permute-start(bf16[192,1536]{1,0:T(8,128)(2,1)S(1)} %get-tuple-element.132.refs_1_), channel_id=1, source_target_pairs={{0,4},{4,0},{8,12},{12,8},{16,20},{20,16},{24,28},{28,24},{1,5},{5... | collective-permute-start | bytes 1769480 | tf_op jit(solution)/shard_map/ppermute | solution.py:236
  194.6 26.6 %collective-permute-start.59 = (bf16[192,1536]{1,0:T(8,128)(2,1)S(1)}, bf16[192,1536]{1,0:T(8,128)(2,1)S(1)}, u32[]{:S(2)}, u32[]{:S(2)}) collective-permute-start(bf16[192,1536]{1,0:T(8,128)(2,1)S(1)} %collective-permute-done.58.refs_1_), channel_id=1, source_target_pairs={{0,4},{4,0},{8,12},{12,8},{16,20},{20,16},{24,28},{28,24},{1,5},{5... | collective-permute-start | bytes 1769480 | tf_op jit(solution)/shard_map/ppermute | solution.py:236
  195.2 27.7 %collective-permute-start.62 = (bf16[192,1536]{1,0:T(8,128)(2,1)S(1)}, bf16[192,1536]{1,0:T(8,128)(2,1)S(1)}, u32[]{:S(2)}, u32[]{:S(2)}) collective-permute-start(bf16[192,1536]{1,0:T(8,128)(2,1)S(1)} %collective-permute-done.57.refs_2_), channel_id=1, source_target_pairs={{0,4},{4,0},{8,12},{12,8},{16,20},{20,16},{24,28},{28,24},{1,5},{5... | collective-permute-start | bytes 1769480 | tf_op jit(solution)/shard_map/ppermute | solution.py:236
  195.2 27.6 %collective-permute-start.63 = (bf16[192,1536]{1,0:T(8,128)(2,1)S(1)}, bf16[192,1536]{1,0:T(8,128)(2,1)S(1)}, u32[]{:S(2)}, u32[]{:S(2)}) collective-permute-start(bf16[192,1536]{1,0:T(8,128)(2,1)S(1)} %collective-permute-done.60.refs_3_), channel_id=1, source_target_pairs={{0,4},{4,0},{8,12},{12,8},{16,20},{20,16},{24,28},{28,24},{1,5},{5... | collective-permute-start | bytes 1769480 | tf_op jit(solution)/shard_map/ppermute | solution.py:236
  195.7 29.6 %collective-permute-start.65 = (bf16[144,1536]{1,0:T(8,128)(2,1)S(1)}, bf16[144,1536]{1,0:T(8,128)(2,1)S(1)}, u32[]{:S(2)}, u32[]{:S(2)}) collective-permute-start(bf16[144,1536]{1,0:T(8,128)(2,1)S(1)} %collective-permute-done.64.refs_1_), channel_id=1, source_target_pairs={{0,4},{4,0},{8,12},{12,8},{16,20},{20,16},{24,28},{28,24},{1,5},{5... | collective-permute-start | bytes 1327112 | tf_op jit(solution)/shard_map/ppermute | solution.py:236
  (42 other events, 457.3 us)

commit v4 on v3

--- a/solution.py
+++ b/solution.py
@@ -15,27 +15,29 @@
 decay_rate = 0.1
 softness = 0.05
 
-UNITS = 16
-CHUNKS = (2, 3, 4, 3, 3, 1)
+UNITS = 48
+CHUNKS = (5, 8, 10, 10, 8, 5, 2)
 LOADS = (
-    ("ca0",),
-    ("oa0", "ca1"),
-    ("cb0", "oa1", "cb5", "oa5"),
-    ("ob0", "ob1", "ca3", "oa3", "ca4", "oa4", "ca5"),
-    ("mm0", "cb1", "ob5"),
-    ("ca2", "oa2", "cb3", "ob3"),
-    ("mm1", "cb2", "ob2", "mm3", "cb4", "ob4", "mm5"),
-    ("mm2", "mm4"),
+    ("ca1", "oa1", "ca6", "oa6"),
+    ("ca0", "cb0", "oa3", "oa4", "ca5", "cb6"),
+    ("cb1", "ca3", "ca4", "oa5", "ob6", "mm6"),
+    ("ob1", "oa2"),
+    ("ob0", "mm1", "ca2", "cb4", "ob4", "cb5"),
+    ("oa0", "mm5"),
+    ("cb3", "ob3", "mm4", "ob5"),
+    ("mm0", "cb2", "ob2", "mm3"),
+    ("mm2",),
 )
 ORDER = (
-    "ld0", "da0", "ld1", "comb0", "R0", "da1", "ld2", "comb1", "R1", "ld3", "da5", "da3", "da4", "comb5",
-    "db0", "sec0", "r0", "comb4", "R5", "comb3", "R3", "ld4", "upd0", "st0", "o0", "R4", "db5", "a0", "db1",
-    "sec1", "r1", "sec5", "r5", "ld5", "da2", "comb2", "R2", "db3", "sec3", "r3", "ld6", "upd1", "st1",
-    "upd5", "b5", "upd3", "st5", "st3", "a5", "db4", "sec4", "r4", "db2", "sec2", "r2", "a1", "a3", "ld7",
-    "upd2", "st2", "upd4", "b3", "o5", "o3", "A0", "f5", "st4", "a4", "b0", "b1", "B3", "A3", "pa3", "F5",
-    "pf5", "f3", "f0", "A5", "a2", "B5", "B0", "pa0", "pa5", "o1", "A1", "B1", "b4", "pa1", "A4", "f1", "F3",
-    "pf3", "o4", "f2", "b2", "B4", "pa4", "o2", "F1", "F0", "pf1", "A2", "f4", "F2", "pf0", "pf2", "B2",
-    "pa2", "F4", "pf4",
+    "ld0", "da6", "da1", "comb6", "R6", "comb1", "R1", "ld1", "db6", "ld2", "sec6", "r6", "da5", "comb5",
+    "R5", "da4", "comb4", "R4", "upd6", "st6", "db1", "da3", "ld3", "sec1", "r1", "comb3", "R3", "o6", "db0",
+    "ld4", "upd1", "st1", "da2", "db4", "sec4", "r4", "ld5", "da0", "comb0", "R0", "db5", "comb2", "ld6",
+    "sec5", "r5", "upd4", "st4", "db3", "b6", "sec3", "r3", "R2", "upd5", "st5", "sec0", "r0", "a6", "ld7",
+    "upd3", "st3", "b1", "upd0", "st0", "a0", "db2", "sec2", "r2", "a1", "b0", "f6", "o0", "a4", "ld8",
+    "upd2", "st2", "B0", "F6", "A1", "f1", "a2", "pf6", "o1", "A0", "b5", "f4", "A4", "f0", "pa0", "F1",
+    "pf1", "b4", "f2", "b2", "F0", "pf0", "o4", "B1", "B4", "pa4", "B6", "F4", "pf4", "a5", "a3", "F2",
+    "pf2", "A6", "pa1", "pa6", "b3", "o3", "o5", "B5", "A5", "B2", "A2", "f3", "A3", "o2", "pa2", "f5", "B3",
+    "pa5", "pa3", "F3", "F5", "pf3", "pf5",
 )
 MOVES = {
     "da": ("ca", "across"),
@@ -101,8 +103,15 @@
         c.wait()
 
 
-def load_kernel(jobs, tile, s_ref, grad_ref, master_ref, momentum_ref, *rest):
+def tile_index():
+    me = lax.axis_index("dp")
+    first = 2 + 2 * (me & 1)
+    return (me, me ^ first, me ^ (6 - first), me ^ 6)
+
+
+def load_kernel(jobs, tile, grad_ref, master_ref, momentum_ref, *rest):
     outs, sem = list(rest[:-1]), rest[-1]
+    index = tile_index()
     pairs = []
     for kind, rows, row0 in jobs:
         if kind == "mm":
@@ -111,18 +120,18 @@
         else:
             dst = outs.pop(0)
             for i, t in enumerate(TILES[kind]):
-                pairs.append((at(grad_ref, (s_ref[t[0]] ^ t[1]) * tile + row0, rows), at(dst, i * rows, rows)))
+                pairs.append((at(grad_ref, (index[t[0]] ^ t[1]) * tile + row0, rows), at(dst, i * rows, rows)))
     run_copies(pairs, sem)
 
 
-def combine_kernel(rows, s_ref, own_ref, peer_ref, out_ref):
+def combine_kernel(rows, own_ref, peer_ref, out_ref):
     def body(row):
         out_ref[pl.ds(row, ROWS), :] = (f32(own_ref, row) + f32(peer_ref, row)).astype(jnp.bfloat16)
 
     rows_loop(2 * rows, body)
 
 
-def second_kernel(rows, s_ref, own_ref, peer_ref, recv_ref, out_ref):
+def second_kernel(rows, own_ref, peer_ref, recv_ref, out_ref):
     def body(row):
         total = f32(own_ref, rows + row) + f32(peer_ref, rows + row) + f32(recv_ref, rows + row)
         out_ref[pl.ds(row, ROWS), :] = total.astype(jnp.bfloat16)
@@ -130,7 +139,7 @@
     rows_loop(rows, body)
 
 
-def update_kernel(rows, scale, s_ref, own_ref, peer_ref, first_ref, second_ref, master_ref, momentum_ref, *outs):
+def update_kernel(rows, scale, own_ref, peer_ref, first_ref, second_ref, master_ref, momentum_ref, *outs):
     new_master_ref, new_momentum_ref, weights_ref = outs
 
     def body(row):
@@ -144,15 +153,16 @@
     rows_loop(rows, body)
 
 
-def place_kernel(which, rows, row0, tile, s_ref, *refs):
+def place_kernel(which, rows, row0, tile, *refs):
+    index = tile_index()
     out_ref, sem = refs[-2:]
     pairs = []
     for src, (i, other) in zip(refs, which):
-        pairs.append((src, at(out_ref, (s_ref[i] ^ other) * tile + row0, rows)))
+        pairs.append((src, at(out_ref, (index[i] ^ other) * tile + row0, rows)))
     run_copies(pairs, sem)
 
 
-def store_kernel(rows, row0, s_ref, master_ref, momentum_ref, *rest):
+def store_kernel(rows, row0, master_ref, momentum_ref, *rest):
     new_master_ref, new_momentum_ref, sem = rest[-3:]
     run_copies([(master_ref, at(new_master_ref, row0, rows)), (momentum_ref, at(new_momentum_ref, row0, rows))], sem)
 
@@ -170,10 +180,6 @@
     grad = grad_parts.reshape(total_rows, cols)
     master = master.reshape(tile, cols)
     momentum = momentum.reshape(tile, cols)
-    me = lax.axis_index("dp")
-    first = jnp.where(me & 1 == 0, 2, 4)
-    second = 6 - first
-    scal = jnp.stack([me, me ^ first, me ^ second, me ^ 6]).astype(jnp.int32)
 
     def first_bit(i):
         return 4 if i & 1 else 2
@@ -187,22 +193,18 @@
     def near(rows, dtype=bf):
         return pltpu.VMEM((rows, cols), dtype)
 
-    def call(kernel, tiles, far, close, outs, copies=0, aliases=None):
+    def call(kernel, far, close, outs, copies=0, aliases=None):
         spaces = [pltpu.HBM] * len(far) + [pltpu.VMEM] * len(close)
         args = [pltpu.with_memory_space_constraint(x, space) for x, space in zip([*far, *close], spaces)]
         return pl.pallas_call(
             kernel,
-            grid_spec=pltpu.PrefetchScalarGridSpec(
-                num_scalar_prefetch=1,
-                grid=(),
-                in_specs=[pl.BlockSpec(memory_space=space) for space in spaces],
-                out_specs=[pl.BlockSpec(memory_space=o.memory_space) for o in outs],
-                scratch_shapes=[pltpu.SemaphoreType.DMA((copies,))] if copies else [],
-            ),
+            in_specs=[pl.BlockSpec(memory_space=space) for space in spaces],
+            out_specs=[pl.BlockSpec(memory_space=o.memory_space) for o in outs],
+            scratch_shapes=[pltpu.SemaphoreType.DMA((copies,))] if copies else [],
             out_shape=outs,
             input_output_aliases=aliases or {},
             compiler_params=pltpu.CompilerParams(vmem_limit_bytes=VMEM_LIMIT),
-        )(tiles, *args)
+        )(*args)
 
     def split(name):
         return name.rstrip(string.digits), int(name.lstrip(string.ascii_letters))
@@ -214,14 +216,14 @@
             outs += [near(sizes[k], jnp.float32)] * 2 if kind == "mm" else [near(2 * sizes[k])]
             copies += 2
         kernel = functools.partial(load_kernel, jobs, tile)
-        got = list(call(kernel, scal, [grad, master, momentum], [], outs, copies))
+        got = list(call(kernel, [grad, master, momentum], [], outs, copies))
         for kind, k in names:
             held[kind, k] = [got.pop(0), got.pop(0)] if kind == "mm" else got.pop(0)
 
     def write(kernel, sources, shapes, finals):
         n = len(finals)
-        body = lambda s_ref, *refs: kernel(s_ref, *refs[n:])
-        got = call(body, scal, finals, sources, shapes, len(sources), {1 + i: i for i in range(n)})
+        body = lambda *refs: kernel(*refs[n:])
+        got = call(body, finals, sources, shapes, len(sources), {i: i for i in range(n)})
         finals[:] = got
 
     weights_shape = [pltpu.HBM((total_rows, cols), bf)]
@@ -238,15 +240,15 @@
             load([split(what) for what in LOADS[k]])
         elif kind == "comb":
             kernel = functools.partial(combine_kernel, rows)
-            (held[kind, k],) = call(kernel, scal, [], get("oa", "da"), [near(2 * rows)])
+            (held[kind, k],) = call(kernel, [], get("oa", "da"), [near(2 * rows)])
         elif kind == "sec":
             kernel = functools.partial(second_kernel, rows)
-            (held[kind, k],) = call(kernel, scal, [], get("ob", "db", "R"), [near(rows)])
+            (held[kind, k],) = call(kernel, [], get("ob", "db", "R"), [near(rows)])
         elif kind == "upd":
             kernel = functools.partial(update_kernel, rows, 1.0 / replicas)
             outs = [near(rows, jnp.float32), near(rows, jnp.float32), near(rows)]
             args = get("ob", "db", "R", "r") + held["mm", k]
-            *held["new", k], held[kind, k] = call(kernel, scal, [], args, outs, 0, {5: 0, 6: 1})
+            *held["new", k], held[kind, k] = call(kernel, [], args, outs, 0, {4: 0, 5: 1})
         elif kind == "st":
             kernel = functools.partial(store_kernel, rows, starts[k])
             write(kernel, held["new", k], state_shape, state)

time: 227 us -> 232 us (1.022)
  Pallas kernels: 68.2 us -> 48.7 us
  waiting for transfers between devices: 111 us -> 124 us
  starting transfers between devices: 46.2 us -> 57.9 us
    pallas_call x44 -> x51, Pallas kernels: 68.2 us -> 48.7 us  [call(): pl.pallas_call(kernel, in_specs=[pl.BlockSpec(memory_space=space) for spa...]
    ppermute x66 -> x77, waiting for transfers between devices: 111 us -> 124 us  [per_device(): held[kind, k] = lax.ppermute(held[source, k], 'dp', perms[how])]
    ppermute x66 -> x77, starting transfers between devices: 46.2 us -> 57.9 us  [per_device(): held[kind, k] = lax.ppermute(held[source, k], 'dp', perms[how])]
  transfers between devices with their start and end apart: 66 -> 77, of which waited for: 18 -> 26; matrix products, arithmetic and copies ran while one was open for 0% -> 0% of each run, Pallas kernels for 28% -> 20%
where the time goes in v4:
time: 232 us
  waiting for transfers between devices  124 us (53%)
  starting transfers between devices  57.9 us (25%)
  Pallas kernels  48.7 us (21%)
    ppermute x77, waiting for transfers between devices, per_device(): held[kind, k] = lax.ppermute(held[source, k], 'dp', perms[how])  124 us
    ppermute x77, starting transfers between devices, per_device(): held[kind, k] = lax.ppermute(held[source, k], 'dp', perms[how])  57.9 us
    pallas_call x51, Pallas kernels, call(): pl.pallas_call(kernel, in_specs=[pl.BlockSpec(memory_space=space) for spa...  48.7 us
  transfers between devices with their start and end apart: 77, of which 26 were waited for; matrix products, arithmetic and copies ran while one was open for 0% of the time, Pallas kernels for 20%

profile of v4, /device:TPU:0, one launch (start us, length us, event | category | flops | bytes accessed | tf_op | source)
XLA Modules:
  0.0 232.0 jit_solution(4722741294048360912)
XLA Ops:
  2.7 2.1 shard_map.59
  5.0 2.6 %shard_map.68 = (bf16[160,1536]{1,0:T(8,128)(2,1)S(1)}, f32[128,1536]{1,0:T(8,128)S(1)}, f32[128,1536]{1,0:T(8,128)S(1)}, bf16[320,1536]{1,0:T(8,128)(2,1)S(1)},...) custom-call(bf16[6144,1536]{1,0:T(8,128)(2,1)} %bitcast.9, ...), custom_call_target="tpu_custom_call" | custom-call | tf_op jit(solution)/shard_map/pallas_call | solution.py:199
  8.8 3.0 %collective-permute-start.2 = (bf16[64,1536]{1,0:T(8,128)(2,1)S(1)}, bf16[64,1536]{1,0:T(8,128)(2,1)S(1)}, u32[]{:S(2)}, u32[]{:S(2)}) collective-permute-start(bf16[64,1536]{1,0:T(8,128)(2,1)S(1)} %shard_map.61), channel_id=1, source_target_pairs={{0,8},{4,20},{8,0},{12,28},{16,24},{20,4},{24,16},{28,12},{1,9},{5... | collective-permute-start | bytes 589832 | tf_op jit(solution)/shard_map/ppermute | solution.py:238
  15.5 2.1 collective-permute-start.3
  17.6 2.6 %collective-permute-done.3.second_ref = bf16[32,1536]{1,0:T(8,128)(2,1)S(1)} collective-permute-done((bf16[32,1536]{1,0:T(8,128)(2,1)S(1)}, bf16[32,1536]{1,0:T(8,128)(2,1)S(1)}, u32[]{:S(2)}, u32[]{:S(2)}) %collective-permute-start.3) | collective-permute-done | bytes 98336 | tf_op jit(solution)/shard_map/ppermute | solution.py:238
  27.6 2.6 %collective-permute-done.55.refs_3_ = bf16[32,1536]{1,0:T(8,128)(2,1)S(1)} collective-permute-done((bf16[32,1536]{1,0:T(8,128)(2,1)S(1)}, bf16[32,1536]{1,0:T(8,128)(2,1)S(1)}, u32[]{:S(2)}, u32[]{:S(2)}) %collective-permute-start.55) | collective-permute-done | bytes 98336 | tf_op jit(solution)/shard_map/ppermute | solution.py:238
  33.5 2.6 %collective-permute-done.29.refs_0_ = bf16[32,1536]{1,0:T(8,128)(2,1)S(1)} collective-permute-done((bf16[32,1536]{1,0:T(8,128)(2,1)S(1)}, bf16[32,1536]{1,0:T(8,128)(2,1)S(1)}, u32[]{:S(2)}, u32[]{:S(2)}) %collective-permute-start.29) | collective-permute-done | bytes 98336 | tf_op jit(solution)/shard_map/ppermute | solution.py:238
  41.4 2.1 shard_map.73
  44.2 2.5 %shard_map.83 = (f32[80,1536]{1,0:T(8,128)S(1)}, f32[80,1536]{1,0:T(8,128)S(1)}, bf16[320,1536]{1,0:T(8,128)(2,1)S(1)}, bf16[320,1536]{1,0:T(8,128)(2,1)S(1)}, f...) custom-call(bf16[6144,1536]{1,0:T(8,128)(2,1)} %bitcast.13, f32[768,1536]{1,0:T(8,128)} %bitcast.22, f32[768,1536]{1,0:T(8,128)} %bitcast.31), custom_call_target="tpu_custom_call" | custom-call | tf_op jit(solution)/shard_map/pallas_call | solution.py:199
  50.3 6.7 %collective-permute-done.14.recv_ref.first_ref = bf16[160,1536]{1,0:T(8,128)(2,1)S(1)} collective-permute-done((bf16[160,1536]{1,0:T(8,128)(2,1)S(1)}, bf16[160,1536]{1,0:T(8,128)(2,1)S(1)}, u32[]{:S(2)}, u32[]{:S(2)}) %collective-permute-start.14) | collective-permute-done | bytes 491552 | tf_op jit(solution)/shard_map/ppermute | solution.py:238
  61.9 4.0 %collective-permute-done.23.second_ref = bf16[80,1536]{1,0:T(8,128)(2,1)S(1)} collective-permute-done((bf16[80,1536]{1,0:T(8,128)(2,1)S(1)}, bf16[80,1536]{1,0:T(8,128)(2,1)S(1)}, u32[]{:S(2)}, u32[]{:S(2)}) %collective-permute-start.23) | collective-permute-done | bytes 245792 | tf_op jit(solution)/shard_map/ppermute | solution.py:238
  71.6 5.6 %collective-permute-done.31.refs_2_ = bf16[80,1536]{1,0:T(8,128)(2,1)S(1)} collective-permute-done((bf16[80,1536]{1,0:T(8,128)(2,1)S(1)}, bf16[80,1536]{1,0:T(8,128)(2,1)S(1)}, u32[]{:S(2)}, u32[]{:S(2)}) %collective-permute-start.31) | collective-permute-done | bytes 245792 | tf_op jit(solution)/shard_map/ppermute | solution.py:238
  78.7 10.4 %collective-permute-done.32.refs_3_ = bf16[80,1536]{1,0:T(8,128)(2,1)S(1)} collective-permute-done((bf16[80,1536]{1,0:T(8,128)(2,1)S(1)}, bf16[80,1536]{1,0:T(8,128)(2,1)S(1)}, u32[]{:S(2)}, u32[]{:S(2)}) %collective-permute-start.32) | collective-permute-done | bytes 245792 | tf_op jit(solution)/shard_map/ppermute | solution.py:238
  92.6 2.7 %collective-permute-done.64.refs_3_ = bf16[80,1536]{1,0:T(8,128)(2,1)S(1)} collective-permute-done((bf16[80,1536]{1,0:T(8,128)(2,1)S(1)}, bf16[80,1536]{1,0:T(8,128)(2,1)S(1)}, u32[]{:S(2)}, u32[]{:S(2)}) %collective-permute-start.64) | collective-permute-done | bytes 245792 | tf_op jit(solution)/shard_map/ppermute | solution.py:238
  101.7 21.6 %collective-permute-done.39.refs_1_ = bf16[80,1536]{1,0:T(8,128)(2,1)S(1)} collective-permute-done((bf16[80,1536]{1,0:T(8,128)(2,1)S(1)}, bf16[80,1536]{1,0:T(8,128)(2,1)S(1)}, u32[]{:S(2)}, u32[]{:S(2)}) %collective-permute-start.39) | collective-permute-done | bytes 245792 | tf_op jit(solution)/shard_map/ppermute | solution.py:238
  127.4 6.3 %collective-permute-done.11.second_ref = bf16[128,1536]{1,0:T(8,128)(2,1)S(1)} collective-permute-done((bf16[128,1536]{1,0:T(8,128)(2,1)S(1)}, bf16[128,1536]{1,0:T(8,128)(2,1)S(1)}, u32[]{:S(2)}, u32[]{:S(2)}) %collective-permute-start.11) | collective-permute-done | bytes 393248 | tf_op jit(solution)/shard_map/ppermute | solution.py:238
  138.5 7.6 %collective-permute-done.41.refs_2_ = bf16[128,1536]{1,0:T(8,128)(2,1)S(1)} collective-permute-done((bf16[128,1536]{1,0:T(8,128)(2,1)S(1)}, bf16[128,1536]{1,0:T(8,128)(2,1)S(1)}, u32[]{:S(2)}, u32[]{:S(2)}) %collective-permute-start.41) | collective-permute-done | bytes 393248 | tf_op jit(solution)/shard_map/ppermute | solution.py:238
  149.4 4.2 %collective-permute-done.51.refs_3_ = bf16[128,1536]{1,0:T(8,128)(2,1)S(1)} collective-permute-done((bf16[128,1536]{1,0:T(8,128)(2,1)S(1)}, bf16[128,1536]{1,0:T(8,128)(2,1)S(1)}, u32[]{:S(2)}, u32[]{:S(2)}) %collective-permute-start.51) | collective-permute-done | bytes 393248 | tf_op jit(solution)/shard_map/ppermute | solution.py:238
  154.1 6.1 %collective-permute-done.19.second_ref = bf16[160,1536]{1,0:T(8,128)(2,1)S(1)} collective-permute-done((bf16[160,1536]{1,0:T(8,128)(2,1)S(1)}, bf16[160,1536]{1,0:T(8,128)(2,1)S(1)}, u32[]{:S(2)}, u32[]{:S(2)}) %collective-permute-start.19) | collective-permute-done | bytes 491552 | tf_op jit(solution)/shard_map/ppermute | solution.py:238
  161.3 8.4 %collective-permute-done.27.second_ref = bf16[160,1536]{1,0:T(8,128)(2,1)S(1)} collective-permute-done((bf16[160,1536]{1,0:T(8,128)(2,1)S(1)}, bf16[160,1536]{1,0:T(8,128)(2,1)S(1)}, u32[]{:S(2)}, u32[]{:S(2)}) %collective-permute-start.27) | collective-permute-done | bytes 491552 | tf_op jit(solution)/shard_map/ppermute | solution.py:238
  177.9 8.9 %collective-permute-done.48.refs_2_ = bf16[160,1536]{1,0:T(8,128)(2,1)S(1)} collective-permute-done((bf16[160,1536]{1,0:T(8,128)(2,1)S(1)}, bf16[160,1536]{1,0:T(8,128)(2,1)S(1)}, u32[]{:S(2)}, u32[]{:S(2)}) %collective-permute-start.48) | collective-permute-done | bytes 491552 | tf_op jit(solution)/shard_map/ppermute | solution.py:238
  189.5 7.9 %collective-permute-done.68.refs_2_ = bf16[160,1536]{1,0:T(8,128)(2,1)S(1)} collective-permute-done((bf16[160,1536]{1,0:T(8,128)(2,1)S(1)}, bf16[160,1536]{1,0:T(8,128)(2,1)S(1)}, u32[]{:S(2)}, u32[]{:S(2)}) %collective-permute-start.68) | collective-permute-done | bytes 491552 | tf_op jit(solution)/shard_map/ppermute | solution.py:238
  199.0 2.7 %collective-permute-done.49.refs_1_ = bf16[160,1536]{1,0:T(8,128)(2,1)S(1)} collective-permute-done((bf16[160,1536]{1,0:T(8,128)(2,1)S(1)}, bf16[160,1536]{1,0:T(8,128)(2,1)S(1)}, u32[]{:S(2)}, u32[]{:S(2)}) %collective-permute-start.49) | collective-permute-done | bytes 491552 | tf_op jit(solution)/shard_map/ppermute | solution.py:238
  203.2 3.7 %collective-permute-done.73.refs_1_ = bf16[160,1536]{1,0:T(8,128)(2,1)S(1)} collective-permute-done((bf16[160,1536]{1,0:T(8,128)(2,1)S(1)}, bf16[160,1536]{1,0:T(8,128)(2,1)S(1)}, u32[]{:S(2)}, u32[]{:S(2)}) %collective-permute-start.73) | collective-permute-done | bytes 491552 | tf_op jit(solution)/shard_map/ppermute | solution.py:238
  (197 shorter events, 101.3 us)
Async XLA Ops:
  20.2 23.3 %collective-permute-start.4 = (bf16[256,1536]{1,0:T(8,128)(2,1)S(1)}, bf16[256,1536]{1,0:T(8,128)(2,1)S(1)}, u32[]{:S(2)}, u32[]{:S(2)}) collective-permute-start(bf16[256,1536]{1,0:T(8,128)(2,1)S(1)} %get-tuple-element.91), channel_id=1, source_target_pairs={{0,4},{4,0},{8,12},{12,8},{16,20},{20,16},{24,28},{28,24},{1,5},{5... | collective-permute-start | bytes 2359304 | tf_op jit(solution)/shard_map/ppermute | solution.py:238
  20.2 23.5 %collective-permute-start.5 = (bf16[256,1536]{1,0:T(8,128)(2,1)S(1)}, bf16[256,1536]{1,0:T(8,128)(2,1)S(1)}, u32[]{:S(2)}, u32[]{:S(2)}) collective-permute-start(bf16[256,1536]{1,0:T(8,128)(2,1)S(1)} %get-tuple-element.93), channel_id=1, source_target_pairs={{0,4},{4,0},{8,12},{12,8},{16,20},{20,16},{24,28},{28,24},{1,5},{5... | collective-permute-start | bytes 2359304 | tf_op jit(solution)/shard_map/ppermute | solution.py:238
  23.0 21.1 %collective-permute-start.8 = (bf16[256,1536]{1,0:T(8,128)(2,1)S(1)}, bf16[256,1536]{1,0:T(8,128)(2,1)S(1)}, u32[]{:S(2)}, u32[]{:S(2)}) collective-permute-start(bf16[256,1536]{1,0:T(8,128)(2,1)S(1)} %get-tuple-element.101), channel_id=1, source_target_pairs={{0,4},{4,0},{8,12},{12,8},{16,20},{20,16},{24,28},{28,24},{1,5},{5... | collective-permute-start | bytes 2359304 | tf_op jit(solution)/shard_map/ppermute | solution.py:238
  23.0 23.7 %collective-permute-start.9 = (bf16[256,1536]{1,0:T(8,128)(2,1)S(1)}, bf16[256,1536]{1,0:T(8,128)(2,1)S(1)}, u32[]{:S(2)}, u32[]{:S(2)}) collective-permute-start(bf16[256,1536]{1,0:T(8,128)(2,1)S(1)} %get-tuple-element.103), channel_id=1, source_target_pairs={{0,4},{4,0},{8,12},{12,8},{16,20},{20,16},{24,28},{28,24},{1,5},{5... | collective-permute-start | bytes 2359304 | tf_op jit(solution)/shard_map/ppermute | solution.py:238
  46.7 21.6 %collective-permute-start.24 = (bf16[320,1536]{1,0:T(8,128)(2,1)S(1)}, bf16[320,1536]{1,0:T(8,128)(2,1)S(1)}, u32[]{:S(2)}, u32[]{:S(2)}) collective-permute-start(bf16[320,1536]{1,0:T(8,128)(2,1)S(1)} %get-tuple-element.141), channel_id=1, source_target_pairs={{0,4},{4,0},{8,12},{12,8},{16,20},{20,16},{24,28},{28,24},{1,5},{5... | collective-permute-start | bytes 2949128 | tf_op jit(solution)/shard_map/ppermute | solution.py:238
  47.7 22.2 %collective-permute-start.25 = (bf16[320,1536]{1,0:T(8,128)(2,1)S(1)}, bf16[320,1536]{1,0:T(8,128)(2,1)S(1)}, u32[]{:S(2)}, u32[]{:S(2)}) collective-permute-start(bf16[320,1536]{1,0:T(8,128)(2,1)S(1)} %get-tuple-element.143), channel_id=1, source_target_pairs={{0,4},{4,0},{8,12},{12,8},{16,20},{20,16},{24,28},{28,24},{1,5},{5... | collective-permute-start | bytes 2949128 | tf_op jit(solution)/shard_map/ppermute | solution.py:238
  59.3 38.4 %collective-permute-start.6 = (bf16[256,1536]{1,0:T(8,128)(2,1)S(1)}, bf16[256,1536]{1,0:T(8,128)(2,1)S(1)}, u32[]{:S(2)}, u32[]{:S(2)}) collective-permute-start(bf16[256,1536]{1,0:T(8,128)(2,1)S(1)} %shard_map.66), channel_id=1, source_target_pairs={{0,8},{4,20},{8,0},{12,28},{16,24},{20,4},{24,16},{28,12},{1,9},{5... | collective-permute-start | bytes 2359304 | tf_op jit(solution)/shard_map/ppermute | solution.py:238
  65.9 33.0 %collective-permute-start.10 = (bf16[256,1536]{1,0:T(8,128)(2,1)S(1)}, bf16[256,1536]{1,0:T(8,128)(2,1)S(1)}, u32[]{:S(2)}, u32[]{:S(2)}) collective-permute-start(bf16[256,1536]{1,0:T(8,128)(2,1)S(1)} %shard_map.71), channel_id=1, source_target_pairs={{0,8},{4,20},{8,0},{12,28},{16,24},{20,4},{24,16},{28,12},{1,9},{5... | collective-permute-start | bytes 2359304 | tf_op jit(solution)/shard_map/ppermute | solution.py:238
  69.9 19.2 %collective-permute-start.32 = (bf16[80,1536]{1,0:T(8,128)(2,1)S(1)}, bf16[80,1536]{1,0:T(8,128)(2,1)S(1)}, u32[]{:S(2)}, u32[]{:S(2)}) collective-permute-start(bf16[80,1536]{1,0:T(8,128)(2,1)S(1)} %get-tuple-element.151.refs_1_), channel_id=1, source_target_pairs={{0,8},{4,20},{8,0},{12,28},{16,24},{20,4},{24,16},{28,12},{1,9},{5... | collective-permute-start | bytes 737288 | tf_op jit(solution)/shard_map/ppermute | solution.py:238
  91.8 44.2 %collective-permute-start.18 = (bf16[320,1536]{1,0:T(8,128)(2,1)S(1)}, bf16[320,1536]{1,0:T(8,128)(2,1)S(1)}, u32[]{:S(2)}, u32[]{:S(2)}) collective-permute-start(bf16[320,1536]{1,0:T(8,128)(2,1)S(1)} %shard_map.81), channel_id=1, source_target_pairs={{0,8},{4,20},{8,0},{12,28},{16,24},{20,4},{24,16},{28,12},{1,9},{5... | collective-permute-start | bytes 2949128 | tf_op jit(solution)/shard_map/ppermute | solution.py:238
  97.7 39.4 %collective-permute-start.26 = (bf16[320,1536]{1,0:T(8,128)(2,1)S(1)}, bf16[320,1536]{1,0:T(8,128)(2,1)S(1)}, u32[]{:S(2)}, u32[]{:S(2)}) collective-permute-start(bf16[320,1536]{1,0:T(8,128)(2,1)S(1)} %shard_map.90), channel_id=1, source_target_pairs={{0,8},{4,20},{8,0},{12,28},{16,24},{20,4},{24,16},{28,12},{1,9},{5... | collective-permute-start | bytes 2949128 | tf_op jit(solution)/shard_map/ppermute | solution.py:238
  98.9 24.4 %collective-permute-start.39 = (bf16[80,1536]{1,0:T(8,128)(2,1)S(1)}, bf16[80,1536]{1,0:T(8,128)(2,1)S(1)}, u32[]{:S(2)}, u32[]{:S(2)}) collective-permute-start(bf16[80,1536]{1,0:T(8,128)(2,1)S(1)} %collective-permute-done.31.refs_2_), channel_id=1, source_target_pairs={{0,8},{4,20},{8,0},{12,28},{16,24},{20,4},{24,16},{28,12},{1,9},{5... | collective-permute-start | bytes 737288 | tf_op jit(solution)/shard_map/ppermute | solution.py:238
  100.0 24.7 %collective-permute-start.7 = (bf16[128,1536]{1,0:T(8,128)(2,1)S(1)}, bf16[128,1536]{1,0:T(8,128)(2,1)S(1)}, u32[]{:S(2)}, u32[]{:S(2)}) collective-permute-start(bf16[128,1536]{1,0:T(8,128)(2,1)S(1)} %shard_map.67), channel_id=1, source_target_pairs={{0,16},{4,12},{8,24},{12,4},{16,0},{20,28},{24,8},{28,20},{1,17},{... | collective-permute-start | bytes 1179656 | tf_op jit(solution)/shard_map/ppermute | solution.py:238
  101.5 23.2 %collective-permute-start.66 = (bf16[80,1536]{1,0:T(8,128)(2,1)S(1)}, bf16[80,1536]{1,0:T(8,128)(2,1)S(1)}, u32[]{:S(2)}, u32[]{:S(2)}) collective-permute-start(bf16[80,1536]{1,0:T(8,128)(2,1)S(1)} %collective-permute-done.63.refs_2_), channel_id=1, source_target_pairs={{0,4},{4,0},{8,12},{12,8},{16,20},{20,16},{24,28},{28,24},{1,5},{5... | collective-permute-start | bytes 737288 | tf_op jit(solution)/shard_map/ppermute | solution.py:238
  147.4 22.3 %collective-permute-start.27 = (bf16[160,1536]{1,0:T(8,128)(2,1)S(1)}, bf16[160,1536]{1,0:T(8,128)(2,1)S(1)}, u32[]{:S(2)}, u32[]{:S(2)}) collective-permute-start(bf16[160,1536]{1,0:T(8,128)(2,1)S(1)} %shard_map.91), channel_id=1, source_target_pairs={{0,16},{4,12},{8,24},{12,4},{16,0},{20,28},{24,8},{28,20},{1,17},{... | collective-permute-start | bytes 1474568 | tf_op jit(solution)/shard_map/ppermute | solution.py:238
  148.2 21.5 %collective-permute-start.37 = (bf16[128,1536]{1,0:T(8,128)(2,1)S(1)}, bf16[128,1536]{1,0:T(8,128)(2,1)S(1)}, u32[]{:S(2)}, u32[]{:S(2)}) collective-permute-start(bf16[128,1536]{1,0:T(8,128)(2,1)S(1)} %collective-permute-done.36.refs_2_), channel_id=1, source_target_pairs={{0,8},{4,20},{8,0},{12,28},{16,24},{20,4},{24,16},{28,12},{1,9},{5... | collective-permute-start | bytes 1179656 | tf_op jit(solution)/shard_map/ppermute | solution.py:238
  153.6 20.5 %collective-permute-start.45 = (bf16[128,1536]{1,0:T(8,128)(2,1)S(1)}, bf16[128,1536]{1,0:T(8,128)(2,1)S(1)}, u32[]{:S(2)}, u32[]{:S(2)}) collective-permute-start(bf16[128,1536]{1,0:T(8,128)(2,1)S(1)} %collective-permute-done.42.refs_3_), channel_id=1, source_target_pairs={{0,4},{4,0},{8,12},{12,8},{16,20},{20,16},{24,28},{28,24},{1,5},{5... | collective-permute-start | bytes 1179656 | tf_op jit(solution)/shard_map/ppermute | solution.py:238
  176.4 21.0 %collective-permute-start.68 = (bf16[160,1536]{1,0:T(8,128)(2,1)S(1)}, bf16[160,1536]{1,0:T(8,128)(2,1)S(1)}, u32[]{:S(2)}, u32[]{:S(2)}) collective-permute-start(bf16[160,1536]{1,0:T(8,128)(2,1)S(1)} %get-tuple-element.156.refs_1_), channel_id=1, source_target_pairs={{0,16},{4,12},{8,24},{12,4},{16,0},{20,28},{24,8},{28,20},{1,17},{... | collective-permute-start | bytes 1474568 | tf_op jit(solution)/shard_map/ppermute | solution.py:238
  177.0 20.4 %collective-permute-start.69 = (bf16[160,1536]{1,0:T(8,128)(2,1)S(1)}, bf16[160,1536]{1,0:T(8,128)(2,1)S(1)}, u32[]{:S(2)}, u32[]{:S(2)}) collective-permute-start(bf16[160,1536]{1,0:T(8,128)(2,1)S(1)} %get-tuple-element.156.refs_1_), channel_id=1, source_target_pairs={{0,8},{4,20},{8,0},{12,28},{16,24},{20,4},{24,16},{28,12},{1,9},{5... | collective-permute-start | bytes 1474568 | tf_op jit(solution)/shard_map/ppermute | solution.py:238
  202.6 24.9 %collective-permute-start.70 = (bf16[160,1536]{1,0:T(8,128)(2,1)S(1)}, bf16[160,1536]{1,0:T(8,128)(2,1)S(1)}, u32[]{:S(2)}, u32[]{:S(2)}) collective-permute-start(bf16[160,1536]{1,0:T(8,128)(2,1)S(1)} %get-tuple-element.156.refs_1_), channel_id=1, source_target_pairs={{0,4},{4,0},{8,12},{12,8},{16,20},{20,16},{24,28},{28,24},{1,5},{5... | collective-permute-start | bytes 1474568 | tf_op jit(solution)/shard_map/ppermute | solution.py:238
  202.6 24.9 %collective-permute-start.71 = (bf16[160,1536]{1,0:T(8,128)(2,1)S(1)}, bf16[160,1536]{1,0:T(8,128)(2,1)S(1)}, u32[]{:S(2)}, u32[]{:S(2)}) collective-permute-start(bf16[160,1536]{1,0:T(8,128)(2,1)S(1)} %collective-permute-done.68.refs_2_), channel_id=1, source_target_pairs={{0,4},{4,0},{8,12},{12,8},{16,20},{20,16},{24,28},{28,24},{1,5},{5... | collective-permute-start | bytes 1474568 | tf_op jit(solution)/shard_map/ppermute | solution.py:238
  203.1 24.4 %collective-permute-start.72 = (bf16[160,1536]{1,0:T(8,128)(2,1)S(1)}, bf16[160,1536]{1,0:T(8,128)(2,1)S(1)}, u32[]{:S(2)}, u32[]{:S(2)}) collective-permute-start(bf16[160,1536]{1,0:T(8,128)(2,1)S(1)} %collective-permute-done.69.refs_3_), channel_id=1, source_target_pairs={{0,4},{4,0},{8,12},{12,8},{16,20},{20,16},{24,28},{28,24},{1,5},{5... | collective-permute-start | bytes 1474568 | tf_op jit(solution)/shard_map/ppermute | solution.py:238
  206.9 22.2 %collective-permute-start.74 = (bf16[160,1536]{1,0:T(8,128)(2,1)S(1)}, bf16[160,1536]{1,0:T(8,128)(2,1)S(1)}, u32[]{:S(2)}, u32[]{:S(2)}) collective-permute-start(bf16[160,1536]{1,0:T(8,128)(2,1)S(1)} %collective-permute-done.73.refs_1_), channel_id=1, source_target_pairs={{0,4},{4,0},{8,12},{12,8},{16,20},{20,16},{24,28},{28,24},{1,5},{5... | collective-permute-start | bytes 1474568 | tf_op jit(solution)/shard_map/ppermute | solution.py:238
  207.6 22.6 %collective-permute-start.76 = (bf16[80,1536]{1,0:T(8,128)(2,1)}, bf16[80,1536]{1,0:T(8,128)(2,1)}, u32[]{:S(2)}, u32[]{:S(2)}) collective-permute-start(bf16[80,1536]{1,0:T(8,128)(2,1)} %collective-permute-done.75.refs_1_), channel_id=1, source_target_pairs={{0,4},{4,0},{8,12},{12,8},{16,20},{20,16},{24,28},{28,24},{1,5},{5... | collective-permute-start | bytes 737288 | tf_op jit(solution)/shard_map/ppermute | solution.py:238
  (61 other events, 550.8 us)
